TPU v7x, 32 devices: a whole 2x2x4 slice. The times are simulated.
32 devices in a mesh: gx: 4 (over y, x), gy: 4 (over z), gz: 2 (over core).
Axes of the slice: x: 2, y: 2, z: 4, core: 2. Of those that a mesh axis runs over, the one named last changes fastest.
Arguments:
- charges: float32 [128, 256, 256], P('gx', 'gy', 'gz'), may hold values from -8 to 8
- kernel_taps: float32 [5, 3, 17], replicated, may hold values from 0.08 to 0.4
Outputs:
- potential: float32 [128, 256, 256], P('gx', 'gy', 'gz')
All inputs are finite; a program needn't handle non-finite values.
Results may differ from a plain program's by a relative error of at most 0.00029.
Values sent between devices are 32-bit elements; how exact they have to be, the bound alone decides.
A program may use at most 128 MiB of HBM per device.

v0:
```python
import functools

import jax
import jax.numpy as jnp
from jax import lax
from jax.experimental import pallas as pl
from jax.experimental.pallas import tpu as pltpu
from jax.sharding import PartitionSpec as P

F32, BF16 = jnp.float32, jnp.bfloat16
LANES = 128
AXES = ("gx", "gy", "gz")
ODD = (-0.0625, 0.5625, 0.5625, -0.0625)
SIDES = tuple((a, b) for a in (-1, 0, 1) for b in (-1, 0, 1) if (a, b) != (0, 0))


def split(v):
    hi = v.astype(BF16)
    return hi, (v - hi.astype(F32)).astype(BF16)


def mm(a, b):
    return jnp.dot(a, b, preferred_element_type=F32)


def exact(a, b):
    return jnp.dot(a, b, preferred_element_type=F32, precision=lax.Precision.HIGHEST)


def dot_right(v, w):
    hi, lo = split(v)
    out = mm(hi, w[0][...]) + mm(lo, w[0][...])
    return out if w[1] is None else out + mm(hi, w[1][...])


def dot_left(w_ref, v, terms):
    hi, lo = split(v)
    return mm(w_ref[...], jnp.concatenate([hi, lo, hi][:terms], axis=0))


def grids(rows, cols):
    return (
        lax.broadcasted_iota(jnp.int32, (rows, cols), 0),
        lax.broadcasted_iota(jnp.int32, (rows, cols), 1),
    )


def pick(taps, level, axis, diff, ok):
    out = jnp.zeros(diff.shape, F32)
    for t in range(17):
        out = jnp.where(diff == t, taps[level, axis, t], out)
    return jnp.where(ok, out, 0.0)


def cubic(diff, ok):
    d = jnp.abs(diff)
    out = jnp.where(d == 0, 1.0, jnp.where(d == 1, 0.5625, jnp.where(d == 3, -0.0625, 0.0)))
    return jnp.where(ok, out, 0.0).astype(F32)


def up(n, m):
    return -(-n // m) * m


def inside(v, n):
    return (v >= 0) & (v < n)


def kernel(counts, dims, taps, x_ref, out_ref, e0, l0, r0, y0, y1, e1, l1, r1, t1, s1, g2, u2, y2, p2, d1,
           w0h, w0l, m0, w1h, w1l, m1, w2h, w2l, m2, c2, pz2, py2, pz1, py1,
           sa, ra, sza, rza, sb, rb, szb, rzb, sg, rg):
    nx, ny, nz = counts
    bx, by, bz = dims
    here = tuple(lax.axis_index(a) for a in AXES)
    gx, gy, gz = here
    cx, cy, cz = bx // 2, by // 2, bz // 2
    fx, fy, fz = bx // 4, by // 4, bz // 4

    def there(dx, dy, dz):
        return inside(gx + dx, nx) & inside(gy + dy, ny) & inside(gz + dz, nz)

    partners = [(a, b, 0) for a, b in SIDES] + [(0, 0, -1), (0, 0, 1)]
    for dim, n in enumerate(counts):
        for d in range(2, n):
            for sgn in (-d, d):
                partners.append(tuple(sgn if k == dim else 0 for k in range(3)))
    barrier = pltpu.get_barrier_semaphore()
    total = jnp.int32(0)
    for p in partners:
        ok = there(*p)
        total = total + ok.astype(jnp.int32)

        @pl.when(ok)
        def _(p=p):
            pl.semaphore_signal(
                barrier, inc=1, device_id=(gx + p[0], gy + p[1], gz + p[2]),
                device_id_type=pl.DeviceIdType.MESH,
            )

    def zero_halo(ref, wx, wy, mx, my):
        for a, b in SIDES:
            @pl.when(jnp.logical_not(there(a, b, 0)))
            def _(a=a, b=b):
                xs = {-1: (0, wx), 0: (wx, mx), 1: (wx + mx, wx)}[a]
                ys = {-1: (0, wy), 0: (wy, my), 1: (wy + my, wy)}[b]
                ref[pl.ds(*xs), pl.ds(*ys), :] = jnp.zeros((xs[1], ys[1], LANES), F32)

    zero_halo(e0, 8, 8, bx, by)
    zero_halo(e1, 5, 16, cx // 2, cy)
    pl.semaphore_wait(barrier, total)

    def exchange(src, base, ref, wx, wy, mx, my, send, recv, near, far=False):
        out = []
        for k, (a, b) in enumerate(SIDES):
            if far and a == 0:
                continue
            rest_x = wx - near
            if far:
                sx = {-1: (near, rest_x), 1: (mx - wx, rest_x)}[a]
                tx = {-1: (wx + mx + near, rest_x), 1: (0, rest_x)}[a]
            else:
                sx = {-1: (0, near), 0: (0, mx), 1: (mx - near, near)}[a]
                tx = {-1: (wx + mx, near), 0: (wx, mx), 1: (wx - near, near)}[a]
            k += len(SIDES) if far else 0
            sy = {-1: (0, wy), 0: (0, my), 1: (my - wy, wy)}[b]
            ty = {-1: (wy + my, wy), 0: (wy, my), 1: (0, wy)}[b]
            copy = pltpu.make_async_remote_copy(
                src_ref=src.at[pl.ds(base[0] + sx[0], sx[1]), pl.ds(base[1] + sy[0], sy[1]), :],
                dst_ref=ref.at[pl.ds(*tx), pl.ds(*ty), :],
                send_sem=send.at[k], recv_sem=recv.at[k],
                device_id=(gx + a, gy + b, gz), device_id_type=pl.DeviceIdType.MESH,
            )
            out.append((there(a, b, 0), there(-a, -b, 0), copy))
        return out

    def across(src, base, left, right, ranges, send, recv):
        out = []
        for k, (ofs, xs, ys) in enumerate(ranges):
            for h, (dz, dst) in enumerate(((1, left), (-1, right))):
                source = (src if k == 0 else base)
                copy = pltpu.make_async_remote_copy(
                    src_ref=source.at[pl.ds(xs[0] - ofs[0], xs[1]), pl.ds(ys[0] - ofs[1], ys[1]), :],
                    dst_ref=dst.at[pl.ds(*xs), pl.ds(*ys), :],
                    send_sem=send.at[k, h], recv_sem=recv.at[k, h],
                    device_id=(gx, gy, gz + dz), device_id_type=pl.DeviceIdType.MESH,
                )
                out.append((there(0, 0, dz), there(0, 0, -dz), copy))
        return out

    def start(copies):
        for to, _, copy in copies:
            pl.when(to)(copy.start)

    def arrive(copies):
        for _, fro, copy in copies:
            pl.when(fro)(copy.wait_recv)

    def left_over(copies):
        for to, _, copy in copies:
            pl.when(to)(copy.wait_send)

    def pieces(wx, wy, mx, my, direct, near):
        o = (wx, wy) if direct else (0, 0)
        n = (0, 0)
        return [
            (o, (wx, mx), (wy, my)),
            (n, (wx - near, near), (0, my + 2 * wy)),
            (n, (wx + mx, near), (0, my + 2 * wy)),
            (n, (wx, mx), (0, wy)),
            (n, (wx, mx), (wy + my, wy)),
            (n, (0, wx - near), (0, my + 2 * wy)),
            (n, (wx + mx + near, wx - near), (0, my + 2 * wy)),
        ]

    xa = exchange(x_ref, (0, 0), e0, 8, 8, bx, by, sa, ra, 4)
    xa_far = exchange(x_ref, (0, 0), e0, 8, 8, bx, by, sa, ra, 4, True)
    za = across(x_ref, e0, l0, r0, pieces(8, 8, bx, by, True, 4), sza, rza)
    start(xa)
    start(za[:2])
    e0[pl.ds(8, bx), pl.ds(8, by), :] = x_ref[...]

    def put(h, l, v):
        hi, lo = split(v)
        h[...] = hi
        if l is not None:
            l[...] = lo

    def stack(ref, v, terms):
        hi, lo = split(v)
        ref[...] = jnp.concatenate([hi, hi, lo][:terms], axis=1)

    i, j = grids(2 * bz, bz)
    pos = jnp.where(i < bz + bz // 2, i, i - 2 * bz)
    k0 = pick(taps, 0, 2, pos - j + 8, inside(pos, bz + 8) | inside(pos + 8, 8))
    rz = cubic(pos - 2 * j, j < cz)
    put(w0h, w0l, jnp.concatenate([k0, rz], axis=1))
    i, j = grids(by + cy, by + 16)
    stack(m0, jnp.where(i < by, pick(taps, 0, 1, j - i, i < by), cubic(j - 8 - 2 * (i - by), i >= by)), 3)
    lane = lax.broadcasted_iota(jnp.int32, (1, LANES), 1)
    flat = [k for k, (a, _) in enumerate(SIDES) if a == 0]
    tilted = [k for k, (a, _) in enumerate(SIDES) if a != 0]
    arrive([xa[k] for k in flat])
    start(za[6:10])
    arrive(za[:2] + za[6:10])

    wide = by + 16
    has_r, has_l = there(0, 0, 1), there(0, 0, -1)
    mask_r, mask_l = (lane < LANES // 2) & has_r, (lane >= LANES // 2) & has_l
    step0 = 4

    def level0(c):
        at = pl.ds(c * step0, step0)
        own = e0[at].reshape(step0 * wide, LANES)
        other = jnp.where(
            mask_r, r0[at].reshape(step0 * wide, LANES),
            jnp.where(mask_l, l0[at].reshape(step0 * wide, LANES), 0.0),
        )
        v = dot_right(jnp.concatenate([own, other], axis=1), (w0h, w0l))
        for k in range(step0):
            o = dot_left(m0, v[k * wide:(k + 1) * wide], 3)
            y0[c * step0 + k] = o[:by, :LANES]
            y1[c * step0 + k] = o[by:, LANES:]

    pl.loop(8 // step0, (8 + bx) // step0)(level0)
    arrive([xa[k] for k in tilted])
    start(za[2:6])
    arrive(za[2:6])
    level0(4 // step0)
    level0((8 + bx) // step0)

    def restrict_x(ref, at):
        return (
            ref[at] + 0.5625 * (ref[at - 1] + ref[at + 1]) - 0.0625 * (ref[at - 3] + ref[at + 3])
        )

    @pl.loop(0, cx // 2)
    def _(p):
        a = restrict_x(y1, 8 + 4 * p)
        b = restrict_x(y1, 10 + 4 * p)
        t1[p] = jnp.where(lane < cz, a, pltpu.roll(b, cz, 1))

    own_copy = pltpu.make_async_copy(t1, e1.at[pl.ds(5, cx // 2), pl.ds(16, cy), :], sg.at[3, 0])
    own_copy.start()
    own_copy.wait()
    xb = exchange(e1, (5, 16), e1, 5, 16, cx // 2, cy, sb, rb, 2)
    xb_far = exchange(e1, (5, 16), e1, 5, 16, cx // 2, cy, sb, rb, 2, True)
    zb = across(e1, e1, l1, r1, pieces(5, 16, cx // 2, cy, False, 2), szb, rzb)
    start(xb)
    start(zb[:2])

    i, j = grids(2 * cz, LANES)
    pos = jnp.where(i < cz + cz // 2, i, i - 2 * cz)
    kk = j - 2
    top = cz + 4
    ok = (j < top) & inside(gz * cz + kk, nz * cz)
    rlane = LANES - fz
    put(w1h, w1l, pick(taps, 1, 2, pos - kk + 8, ok) + cubic(pos - 2 * (j - rlane), j >= rlane))
    ry1 = up(cy + 4, 8)
    i, j = grids(ry1 + fy, cy + 32)
    ok = (i < cy + 4) & inside(gy * cy + i - 2, ny * cy)
    stack(m1, pick(taps, 1, 1, j - 16 - (i - 2) + 8, ok) + cubic(j - 16 - 2 * (i - ry1), i >= ry1), 3)

    arrive([xb[k] for k in flat])
    start(zb[6:10])
    arrive(zb[:2] + zb[6:10])

    half = lax.rem(lane, cz) < cz // 2

    def level1(p):
        own = e1[p]
        other = jnp.where(half & has_r, r1[p], jnp.where(jnp.logical_not(half) & has_l, l1[p], 0.0))
        even = jnp.where(lane < cz, own, pltpu.roll(other, cz, 1))
        odd = jnp.where(lane < cz, pltpu.roll(own, cz, 1), other)
        h = own.shape[0]
        v = dot_right(jnp.concatenate([even, odd], axis=0), (w1h, w1l))
        o = dot_left(m1, jnp.concatenate([v[:h], v[h:]], axis=1), 3)
        s1[2 * p] = o[:, :LANES]
        s1[2 * p + 1] = o[:, LANES:]

    pl.loop(5, 5 + cx // 2)(level1)
    arrive([xb[k] for k in tilted])
    start(zb[2:6])
    arrive(zb[2:6])
    pl.loop(3, 5)(level1)
    pl.loop(5 + cx // 2, 7 + cx // 2)(level1)

    per = LANES // fz
    def restrict_1(q):
        at = 10 + 2 * q
        rows = pl.ds(ry1, fy)
        v = (
            s1[at, rows] + 0.5625 * (s1[at - 1, rows] + s1[at + 1, rows])
            - 0.0625 * (s1[at - 3, rows] + s1[at + 3, rows])
        )
        return jnp.where(lane >= rlane, v, 0.0)

    np2 = fx // per
    for p in range(np2):
        acc = None
        for k in range(per):
            v = restrict_1(p * per + k)
            sh = (fz * k + LANES - rlane) % LANES
            v = pltpu.roll(v, sh, 1) if sh else v
            acc = v if acc is None else acc + v
        p2[p] = acc
    own_copy = pltpu.make_async_copy(p2, g2.at[gz, gy, pl.ds(gx * np2, np2)], sg.at[3, 1])
    own_copy.start()
    own_copy.wait()

    def spread(dim, n, ref, k0):
        out = []
        for m, d in enumerate([d for d in range(-(n - 1), n) if d]):
            dev = tuple(here[k] + (d if k == dim else 0) for k in range(3))
            copy = pltpu.make_async_remote_copy(
                src_ref=ref(here[dim]), dst_ref=ref(here[dim]),
                send_sem=sg.at[dim, m], recv_sem=rg.at[dim, m],
                device_id=dev, device_id_type=pl.DeviceIdType.MESH,
            )
            land = pltpu.make_async_remote_copy(
                src_ref=ref(here[dim]), dst_ref=ref(here[dim] - d),
                send_sem=sg.at[dim, m], recv_sem=rg.at[dim, m],
                device_id=dev, device_id_type=pl.DeviceIdType.MESH,
            )
            to = inside(here[dim] + d, n)
            fro = inside(here[dim] - d, n)
            out.append((to, fro, copy, land))
        return out

    def begin(copies):
        for to, _, copy, _ in copies:
            pl.when(to)(copy.start)

    def landed(copies):
        for _, fro, _, land in copies:
            pl.when(fro)(land.wait_recv)

    ca = spread(0, nx, lambda k: g2.at[gz, gy, pl.ds(k * np2, np2)], 0)
    begin(ca)
    start(xa_far)
    start(xb_far)
    def plain(axis, level, n, pad, turned):
        i, j = grids(pad, pad)
        d = (i - j if turned else j - i) + 8
        return pick(taps, level, axis, d, (i < n) & (j < n))

    def rest(n, pad, big, turned_r):
        i, j = grids(*((big, pad) if turned_r else (pad, big)))
        c, f = (j, i) if turned_r else (i, j)
        return cubic(f - 2 * c, (c < n) & (f < 2 * n))

    def operators(axis, n2, first, rows, count):
        n3, n4 = n2 // 2, n2 // 4
        q = up(n2, LANES)
        i, j = grids(rows, q)
        g = first + i
        ok = (i < count) & inside(g, n2)
        one = pick(taps, 2, axis, j - g + 8, ok & (j < n2))
        pr = cubic(g - 2 * j, ok & (j < n3))
        r23, r34 = rest(n3, q, q, False), rest(n4, q, q, False)
        p34 = rest(n4, q, q, True)
        two = exact(exact(pr, plain(axis, 3, n3, q, False)), r23)
        three = exact(exact(exact(exact(pr, p34), plain(axis, 4, n4, q, False)), r34), r23)
        return one, two, three

    n2x, n2y, n2z = nx * fx, ny * fy, nz * fz
    ez, ey, ex = fz + 5, fy + 5, fx + 5
    tz = 40
    ops = operators(2, n2z, gz * fz - 2, tz, ez)
    cols = jnp.concatenate(list(ops) + [jnp.zeros((LANES - 3 * tz, ops[0].shape[1]), F32)], axis=0)
    put(w2h, w2l, cols.T)
    ty = up(ey, 8)
    ops = operators(1, n2y, gy * fy - 2, ty, ey)
    stack(m2, jnp.concatenate(list(ops), axis=0)[:, :n2y], 3)
    tx = up(ex, 8)
    ops = operators(0, n2x, gx * fx - 2, tx, ex)
    tall = [o.T for o in ops]
    for r in range(ex):
        a, b, c = (o[:n2x, r:r + 1] for o in tall)
        c2[r] = jnp.where(lane < tz, a, jnp.where(lane < 2 * tz, b, c))
    i, j = grids(LANES, LANES)
    src = i - jnp.where(i < tz, 0, jnp.where(i < 2 * tz, tz, 2 * tz)) - 2
    put(pz2, None, cubic((j - 2) - 2 * src, (i < 3 * tz) & (src < fz + 3) & (j < top) & inside(gz * cz + j - 2, nz * cz)))
    i, j = grids(ry1, up(ty, 16))
    stack(py2, cubic((i - 2) - 2 * (j - 2), (j < ey) & (i < cy + 4) & inside(gy * cy + i - 2, ny * cy)), 2)
    i, j = grids(LANES, bz)
    put(pz1, None, cubic(j - 2 * (i - 2), i < top))
    i, j = grids(by, up(ry1, 16))
    stack(py1, cubic(i - 2 * (j - 2), j < cy + 4), 2)

    landed(ca)
    cb = spread(1, ny, lambda k: g2.at[gz, k], 0)
    begin(cb)
    arrive(xa_far)
    start(za[10:])
    arrive(xb_far)
    start(zb[10:])
    arrive(za[10:])
    level0(0)
    level0((12 + bx) // step0)
    arrive(zb[10:])
    pl.loop(0, 3)(level1)
    pl.loop(7 + cx // 2, 10 + cx // 2)(level1)

    seen = lambda r: inside(gx * cx + r - 2, nx * cx).astype(F32)

    @pl.loop(0, cx + 4)
    def _(p):
        rows = pl.ds(0, ry1)
        acc = taps[1, 0, 0] * s1[p, rows]
        for t in range(1, 17):
            acc = acc + taps[1, 0, t] * s1[p + t, rows]
        d1[p] = acc

    @pl.loop(0, bx)
    def _(p):
        acc = taps[0, 0, 0] * y0[p]
        for t in range(1, 17):
            acc = acc + taps[0, 0, t] * y0[p + t]
        out_ref[p] = acc

    landed(cb)
    cc = spread(2, nz, lambda k: g2.at[k], 0)
    begin(cc)
    landed(cc)

    tiles = u2.shape[0]

    @pl.loop(0, nx * np2)
    def _(p):
        for b in range(ny):
            for k in range(per):
                for t in range(tiles):
                    acc = jnp.zeros((fy, LANES), F32)
                    for s in range(t * per, min(nz, (t + 1) * per)):
                        v = g2[s, b, p]
                        sh = (fz * (s - t * per - k)) % LANES
                        v = pltpu.roll(v, sh, 1) if sh else v
                        lo = fz * (s - t * per)
                        acc = jnp.where((lane >= lo) & (lane < lo + fz), v, acc)
                    u2[t, p * per + k, pl.ds(b * fy, fy), :] = acc

    step2 = 2

    @pl.loop(0, n2x // step2)
    def _(c):
        at = pl.ds(c * step2, step2)
        v = jnp.concatenate([u2[t, at].reshape(step2 * n2y, LANES) for t in range(tiles)], axis=1)
        v = dot_right(v, (w2h, w2l))
        v = jnp.concatenate([v[k * n2y:(k + 1) * n2y] for k in range(step2)], axis=1)
        o = dot_left(m2, v, 3)
        for k in range(step2):
            w = o[:, k * LANES:(k + 1) * LANES]
            y2[c * step2 + k] = jnp.where(
                lane < tz, w[:ty], jnp.where(lane < 2 * tz, w[ty:2 * ty], w[2 * ty:])
            )

    parts = []
    for r in range(ex):
        acc = c2[r, pl.ds(0, 1)] * y2[0]
        for q in range(1, n2x):
            acc = acc + c2[r, pl.ds(q, 1)] * y2[q]
        parts.append(acc)
    v = dot_right(jnp.concatenate(parts, axis=0), (pz2, None))
    fill = up(ty, 16) - ty
    pro = []
    for r in range(ex):
        w = v[r * ty:(r + 1) * ty]
        if fill:
            w = jnp.concatenate([w, jnp.zeros((fill, LANES), F32)], axis=0)
        pro.append(dot_left(py2, w, 2))
    for p in range(cx + 4):
        m = (p - 2) // 2 + 2
        if p % 2 == 0:
            w = pro[m]
        else:
            w = 0.5625 * (pro[m] + pro[m + 1]) - 0.0625 * (pro[m - 1] + pro[m + 2])
        d1[p] = (d1[p] + w) * seen(p)

    fill1 = up(ry1, 16) - ry1

    @pl.loop(0, (cx + 4) // 2)
    def _(c):
        v = dot_right(d1[pl.ds(2 * c, 2)].reshape(2 * ry1, LANES), (pz1, None))
        v = jnp.concatenate([v[:ry1], v[ry1:]], axis=1)
        if fill1:
            v = jnp.concatenate([v, jnp.zeros((fill1, 2 * LANES), F32)], axis=0)
        o = dot_left(py1, v, 2)
        y0[2 * c] = o[:, :LANES]
        y0[2 * c + 1] = o[:, LANES:]

    @pl.loop(0, cx)
    def _(m):
        at = m + 2
        out_ref[2 * m] = out_ref[2 * m] + y0[at]
        out_ref[2 * m + 1] = out_ref[2 * m + 1] + (
            0.5625 * (y0[at] + y0[at + 1]) - 0.0625 * (y0[at - 1] + y0[at + 2])
        )

    for group in (xa, xa_far, za, xb, xb_far, zb):
        left_over(group)
    for group in (ca, cb, cc):
        for to, _, copy, _ in group:
            pl.when(to)(copy.wait_send)


def per_device(counts, charges, kernel_taps):
    nx, ny, nz = counts
    bx, by, bz = dims = charges.shape
    assert bz == LANES
    cx, cy, cz = bx // 2, by // 2, bz // 2
    fx, fy, fz = bx // 4, by // 4, bz // 4
    n2x, n2y, n2z = nx * fx, ny * fy, nz * fz
    np2 = fx // (LANES // fz)
    ry1 = up(cy + 4, 8)
    ty = up(fy + 5, 8)
    tiles = up(n2z, LANES) // LANES
    V = pltpu.VMEM
    ext0 = (bx + 16, by + 16, LANES)
    ext1 = (cx // 2 + 10, cy + 32, LANES)
    wide = max(nx, ny, nz) * 2
    dma = pltpu.SemaphoreType.DMA
    scratch = [
        V(ext0, F32), V(ext0, F32), V(ext0, F32),
        V((bx + 16, by, LANES), F32), V((bx + 16, cy, LANES), F32),
        V(ext1, F32), V(ext1, F32), V(ext1, F32),
        V((cx // 2, cy, LANES), F32),
        V((cx + 20, ry1 + fy, LANES), F32),
        V((nz, ny, nx * np2, fy, LANES), F32),
        V((tiles, n2x, n2y, LANES), F32),
        V((n2x, ty, LANES), F32), V((np2, fy, LANES), F32), V((cx + 4, ry1, LANES), F32),
        V((2 * bz, bz + LANES), BF16), V((2 * bz, bz + LANES), BF16),
        V((by + cy, 3 * (by + 16)), BF16),
        V((2 * cz, LANES), BF16), V((2 * cz, LANES), BF16),
        V((ry1 + fy, 3 * (cy + 32)), BF16),
        V((tiles * LANES, LANES), BF16), V((tiles * LANES, LANES), BF16),
        V((3 * ty, 3 * n2y), BF16),
        V((fx + 5, n2x, LANES), F32),
        V((LANES, LANES), BF16), V((ry1, 2 * up(ty, 16)), BF16),
        V((LANES, bz), BF16), V((by, 2 * up(ry1, 16)), BF16),
        dma((16,)), dma((16,)), dma((7, 2)), dma((7, 2)),
        dma((16,)), dma((16,)), dma((7, 2)), dma((7, 2)),
        dma((4, wide)), dma((3, wide)),
    ]
    return pl.pallas_call(
        functools.partial(kernel, counts, dims),
        out_shape=jax.ShapeDtypeStruct(dims, F32),
        in_specs=[pl.BlockSpec(memory_space=pltpu.SMEM), pl.BlockSpec(memory_space=pltpu.VMEM)],
        out_specs=pl.BlockSpec(memory_space=pltpu.VMEM),
        scratch_shapes=scratch,
        compiler_params=pltpu.CompilerParams(
            collective_id=0, has_side_effects=True, vmem_limit_bytes=60 * 2**20
        ),
    )(kernel_taps, charges)


def solution(mesh):
    counts = tuple(mesh.shape[a] for a in AXES)
    return jax.shard_map(
        functools.partial(per_device, counts), mesh=mesh,
        in_specs=(P("gx", "gy", "gz"), P()), out_specs=P("gx", "gy", "gz"), check_vma=False,
    )
```

profile of v0, /device:TPU:0, one launch (start us, length us, event | category | flops | bytes accessed | tf_op | source)
XLA Modules:
  0.0 64.4 jit_solution(10184174212467308997)
XLA Ops:
  0.0 62.0 %shard_map.28 = f32[32,64,128]{2,1,0:T(8,128)} custom-call(f32[5,3,17]{2,1,0:T(4,128)} %taps.1, f32[32,64,128]{2,1,0:T(8,128)} %x_ref.1), custom_call_target="tpu_custom_call" | custom-call | tf_op jit(solution)/shard_map/pallas_call | solution.py:544
  62.0 2.3 %copy.4 = f32[32,64,128]{2,1,0:T(8,128)} copy(f32[32,64,128]{2,1,0:T(8,128)} %shard_map.28) | data formatting | bytes 2097152
where the time goes:
time: 64.6 us; the launch traced here: 64.4 us
  Pallas kernels  62 us (96%)
  local copies, waits for them, and re-layouts  2.31 us (4%)
    pallas_call x1, Pallas kernels, per_device(): pl.pallas_call(functools.partial(kernel, counts, dims), out_shape=jax.Sha...  62 us
    unnamed x1, local copies, waits for them, and re-layouts  2.31 us

commit v1 on v0

--- a/solution.py
+++ b/solution.py
@@ -9,6 +9,7 @@
 
 F32, BF16 = jnp.float32, jnp.bfloat16
 LANES = 128
+U0, U1, U2, U3 = 4, 4, 4, 5
 AXES = ("gx", "gy", "gz")
 ODD = (-0.0625, 0.5625, 0.5625, -0.0625)
 SIDES = tuple((a, b) for a in (-1, 0, 1) for b in (-1, 0, 1) if (a, b) != (0, 0))
@@ -197,57 +198,6 @@
     i, j = grids(by + cy, by + 16)
     stack(m0, jnp.where(i < by, pick(taps, 0, 1, j - i, i < by), cubic(j - 8 - 2 * (i - by), i >= by)), 3)
     lane = lax.broadcasted_iota(jnp.int32, (1, LANES), 1)
-    flat = [k for k, (a, _) in enumerate(SIDES) if a == 0]
-    tilted = [k for k, (a, _) in enumerate(SIDES) if a != 0]
-    arrive([xa[k] for k in flat])
-    start(za[6:10])
-    arrive(za[:2] + za[6:10])
-
-    wide = by + 16
-    has_r, has_l = there(0, 0, 1), there(0, 0, -1)
-    mask_r, mask_l = (lane < LANES // 2) & has_r, (lane >= LANES // 2) & has_l
-    step0 = 4
-
-    def level0(c):
-        at = pl.ds(c * step0, step0)
-        own = e0[at].reshape(step0 * wide, LANES)
-        other = jnp.where(
-            mask_r, r0[at].reshape(step0 * wide, LANES),
-            jnp.where(mask_l, l0[at].reshape(step0 * wide, LANES), 0.0),
-        )
-        v = dot_right(jnp.concatenate([own, other], axis=1), (w0h, w0l))
-        for k in range(step0):
-            o = dot_left(m0, v[k * wide:(k + 1) * wide], 3)
-            y0[c * step0 + k] = o[:by, :LANES]
-            y1[c * step0 + k] = o[by:, LANES:]
-
-    pl.loop(8 // step0, (8 + bx) // step0)(level0)
-    arrive([xa[k] for k in tilted])
-    start(za[2:6])
-    arrive(za[2:6])
-    level0(4 // step0)
-    level0((8 + bx) // step0)
-
-    def restrict_x(ref, at):
-        return (
-            ref[at] + 0.5625 * (ref[at - 1] + ref[at + 1]) - 0.0625 * (ref[at - 3] + ref[at + 3])
-        )
-
-    @pl.loop(0, cx // 2)
-    def _(p):
-        a = restrict_x(y1, 8 + 4 * p)
-        b = restrict_x(y1, 10 + 4 * p)
-        t1[p] = jnp.where(lane < cz, a, pltpu.roll(b, cz, 1))
-
-    own_copy = pltpu.make_async_copy(t1, e1.at[pl.ds(5, cx // 2), pl.ds(16, cy), :], sg.at[3, 0])
-    own_copy.start()
-    own_copy.wait()
-    xb = exchange(e1, (5, 16), e1, 5, 16, cx // 2, cy, sb, rb, 2)
-    xb_far = exchange(e1, (5, 16), e1, 5, 16, cx // 2, cy, sb, rb, 2, True)
-    zb = across(e1, e1, l1, r1, pieces(5, 16, cx // 2, cy, False, 2), szb, rzb)
-    start(xb)
-    start(zb[:2])
-
     i, j = grids(2 * cz, LANES)
     pos = jnp.where(i < cz + cz // 2, i, i - 2 * cz)
     kk = j - 2
@@ -260,84 +210,6 @@
     ok = (i < cy + 4) & inside(gy * cy + i - 2, ny * cy)
     stack(m1, pick(taps, 1, 1, j - 16 - (i - 2) + 8, ok) + cubic(j - 16 - 2 * (i - ry1), i >= ry1), 3)
 
-    arrive([xb[k] for k in flat])
-    start(zb[6:10])
-    arrive(zb[:2] + zb[6:10])
-
-    half = lax.rem(lane, cz) < cz // 2
-
-    def level1(p):
-        own = e1[p]
-        other = jnp.where(half & has_r, r1[p], jnp.where(jnp.logical_not(half) & has_l, l1[p], 0.0))
-        even = jnp.where(lane < cz, own, pltpu.roll(other, cz, 1))
-        odd = jnp.where(lane < cz, pltpu.roll(own, cz, 1), other)
-        h = own.shape[0]
-        v = dot_right(jnp.concatenate([even, odd], axis=0), (w1h, w1l))
-        o = dot_left(m1, jnp.concatenate([v[:h], v[h:]], axis=1), 3)
-        s1[2 * p] = o[:, :LANES]
-        s1[2 * p + 1] = o[:, LANES:]
-
-    pl.loop(5, 5 + cx // 2)(level1)
-    arrive([xb[k] for k in tilted])
-    start(zb[2:6])
-    arrive(zb[2:6])
-    pl.loop(3, 5)(level1)
-    pl.loop(5 + cx // 2, 7 + cx // 2)(level1)
-
-    per = LANES // fz
-    def restrict_1(q):
-        at = 10 + 2 * q
-        rows = pl.ds(ry1, fy)
-        v = (
-            s1[at, rows] + 0.5625 * (s1[at - 1, rows] + s1[at + 1, rows])
-            - 0.0625 * (s1[at - 3, rows] + s1[at + 3, rows])
-        )
-        return jnp.where(lane >= rlane, v, 0.0)
-
-    np2 = fx // per
-    for p in range(np2):
-        acc = None
-        for k in range(per):
-            v = restrict_1(p * per + k)
-            sh = (fz * k + LANES - rlane) % LANES
-            v = pltpu.roll(v, sh, 1) if sh else v
-            acc = v if acc is None else acc + v
-        p2[p] = acc
-    own_copy = pltpu.make_async_copy(p2, g2.at[gz, gy, pl.ds(gx * np2, np2)], sg.at[3, 1])
-    own_copy.start()
-    own_copy.wait()
-
-    def spread(dim, n, ref, k0):
-        out = []
-        for m, d in enumerate([d for d in range(-(n - 1), n) if d]):
-            dev = tuple(here[k] + (d if k == dim else 0) for k in range(3))
-            copy = pltpu.make_async_remote_copy(
-                src_ref=ref(here[dim]), dst_ref=ref(here[dim]),
-                send_sem=sg.at[dim, m], recv_sem=rg.at[dim, m],
-                device_id=dev, device_id_type=pl.DeviceIdType.MESH,
-            )
-            land = pltpu.make_async_remote_copy(
-                src_ref=ref(here[dim]), dst_ref=ref(here[dim] - d),
-                send_sem=sg.at[dim, m], recv_sem=rg.at[dim, m],
-                device_id=dev, device_id_type=pl.DeviceIdType.MESH,
-            )
-            to = inside(here[dim] + d, n)
-            fro = inside(here[dim] - d, n)
-            out.append((to, fro, copy, land))
-        return out
-
-    def begin(copies):
-        for to, _, copy, _ in copies:
-            pl.when(to)(copy.start)
-
-    def landed(copies):
-        for _, fro, _, land in copies:
-            pl.when(fro)(land.wait_recv)
-
-    ca = spread(0, nx, lambda k: g2.at[gz, gy, pl.ds(k * np2, np2)], 0)
-    begin(ca)
-    start(xa_far)
-    start(xb_far)
     def plain(axis, level, n, pad, turned):
         i, j = grids(pad, pad)
         d = (i - j if turned else j - i) + 8
@@ -387,6 +259,135 @@
     i, j = grids(by, up(ry1, 16))
     stack(py1, cubic(i - 2 * (j - 2), j < cy + 4), 2)
 
+    flat = [k for k, (a, _) in enumerate(SIDES) if a == 0]
+    tilted = [k for k, (a, _) in enumerate(SIDES) if a != 0]
+    arrive([xa[k] for k in flat])
+    start(za[6:10])
+    arrive(za[:2] + za[6:10])
+
+    wide = by + 16
+    has_r, has_l = there(0, 0, 1), there(0, 0, -1)
+    mask_r, mask_l = (lane < LANES // 2) & has_r, (lane >= LANES // 2) & has_l
+    step0 = 4
+
+    def level0(c):
+        at = pl.ds(c * step0, step0)
+        own = e0[at].reshape(step0 * wide, LANES)
+        other = jnp.where(
+            mask_r, r0[at].reshape(step0 * wide, LANES),
+            jnp.where(mask_l, l0[at].reshape(step0 * wide, LANES), 0.0),
+        )
+        v = dot_right(jnp.concatenate([own, other], axis=1), (w0h, w0l))
+        for k in range(step0):
+            o = dot_left(m0, v[k * wide:(k + 1) * wide], 3)
+            y0[c * step0 + k] = o[:by, :LANES]
+            y1[c * step0 + k] = o[by:, LANES:]
+
+    pl.loop(8 // step0, (8 + bx) // step0, unroll=U0)(level0)
+    arrive([xa[k] for k in tilted])
+    start(za[2:6])
+    arrive(za[2:6])
+    level0(4 // step0)
+    level0((8 + bx) // step0)
+
+    def restrict_x(ref, at):
+        return (
+            ref[at] + 0.5625 * (ref[at - 1] + ref[at + 1]) - 0.0625 * (ref[at - 3] + ref[at + 3])
+        )
+
+    @pl.loop(0, cx // 2)
+    def _(p):
+        a = restrict_x(y1, 8 + 4 * p)
+        b = restrict_x(y1, 10 + 4 * p)
+        t1[p] = jnp.where(lane < cz, a, pltpu.roll(b, cz, 1))
+
+    own_copy = pltpu.make_async_copy(t1, e1.at[pl.ds(5, cx // 2), pl.ds(16, cy), :], sg.at[3, 0])
+    own_copy.start()
+    own_copy.wait()
+    xb = exchange(e1, (5, 16), e1, 5, 16, cx // 2, cy, sb, rb, 2)
+    xb_far = exchange(e1, (5, 16), e1, 5, 16, cx // 2, cy, sb, rb, 2, True)
+    zb = across(e1, e1, l1, r1, pieces(5, 16, cx // 2, cy, False, 2), szb, rzb)
+    start(xb)
+    start(zb[:2])
+    start(xa_far)
+    start(xb_far)
+
+    arrive([xb[k] for k in flat])
+    start(zb[6:10])
+    arrive(zb[:2] + zb[6:10])
+
+    half = lax.rem(lane, cz) < cz // 2
+
+    def level1(p):
+        own = e1[p]
+        other = jnp.where(half & has_r, r1[p], jnp.where(jnp.logical_not(half) & has_l, l1[p], 0.0))
+        even = jnp.where(lane < cz, own, pltpu.roll(other, cz, 1))
+        odd = jnp.where(lane < cz, pltpu.roll(own, cz, 1), other)
+        h = own.shape[0]
+        v = dot_right(jnp.concatenate([even, odd], axis=0), (w1h, w1l))
+        o = dot_left(m1, jnp.concatenate([v[:h], v[h:]], axis=1), 3)
+        s1[2 * p] = o[:, :LANES]
+        s1[2 * p + 1] = o[:, LANES:]
+
+    pl.loop(5, 5 + cx // 2, unroll=U1)(level1)
+    arrive([xb[k] for k in tilted])
+    start(zb[2:6])
+    arrive(zb[2:6])
+    pl.loop(3, 5, unroll=True)(level1)
+    pl.loop(5 + cx // 2, 7 + cx // 2, unroll=True)(level1)
+
+    per = LANES // fz
+    def restrict_1(q):
+        at = 10 + 2 * q
+        rows = pl.ds(ry1, fy)
+        v = (
+            s1[at, rows] + 0.5625 * (s1[at - 1, rows] + s1[at + 1, rows])
+            - 0.0625 * (s1[at - 3, rows] + s1[at + 3, rows])
+        )
+        return jnp.where(lane >= rlane, v, 0.0)
+
+    np2 = fx // per
+    for p in range(np2):
+        acc = None
+        for k in range(per):
+            v = restrict_1(p * per + k)
+            sh = (fz * k + LANES - rlane) % LANES
+            v = pltpu.roll(v, sh, 1) if sh else v
+            acc = v if acc is None else acc + v
+        p2[p] = acc
+    own_copy = pltpu.make_async_copy(p2, g2.at[gz, gy, pl.ds(gx * np2, np2)], sg.at[3, 1])
+    own_copy.start()
+    own_copy.wait()
+
+    def spread(dim, n, ref, k0):
+        out = []
+        for m, d in enumerate([d for d in range(-(n - 1), n) if d]):
+            dev = tuple(here[k] + (d if k == dim else 0) for k in range(3))
+            copy = pltpu.make_async_remote_copy(
+                src_ref=ref(here[dim]), dst_ref=ref(here[dim]),
+                send_sem=sg.at[dim, m], recv_sem=rg.at[dim, m],
+                device_id=dev, device_id_type=pl.DeviceIdType.MESH,
+            )
+            land = pltpu.make_async_remote_copy(
+                src_ref=ref(here[dim]), dst_ref=ref(here[dim] - d),
+                send_sem=sg.at[dim, m], recv_sem=rg.at[dim, m],
+                device_id=dev, device_id_type=pl.DeviceIdType.MESH,
+            )
+            to = inside(here[dim] + d, n)
+            fro = inside(here[dim] - d, n)
+            out.append((to, fro, copy, land))
+        return out
+
+    def begin(copies):
+        for to, _, copy, _ in copies:
+            pl.when(to)(copy.start)
+
+    def landed(copies):
+        for _, fro, _, land in copies:
+            pl.when(fro)(land.wait_recv)
+
+    ca = spread(0, nx, lambda k: g2.at[gz, gy, pl.ds(k * np2, np2)], 0)
+    begin(ca)
     landed(ca)
     cb = spread(1, ny, lambda k: g2.at[gz, k], 0)
     begin(cb)
@@ -398,8 +399,8 @@
     level0(0)
     level0((12 + bx) // step0)
     arrive(zb[10:])
-    pl.loop(0, 3)(level1)
-    pl.loop(7 + cx // 2, 10 + cx // 2)(level1)
+    pl.loop(0, 3, unroll=True)(level1)
+    pl.loop(7 + cx // 2, 10 + cx // 2, unroll=True)(level1)
 
     seen = lambda r: inside(gx * cx + r - 2, nx * cx).astype(F32)
 
@@ -441,7 +442,7 @@
 
     step2 = 2
 
-    @pl.loop(0, n2x // step2)
+    @pl.loop(0, n2x // step2, unroll=U2)
     def _(c):
         at = pl.ds(c * step2, step2)
         v = jnp.concatenate([u2[t, at].reshape(step2 * n2y, LANES) for t in range(tiles)], axis=1)
@@ -478,7 +479,7 @@
 
     fill1 = up(ry1, 16) - ry1
 
-    @pl.loop(0, (cx + 4) // 2)
+    @pl.loop(0, (cx + 4) // 2, unroll=U3)
     def _(c):
         v = dot_right(d1[pl.ds(2 * c, 2)].reshape(2 * ry1, LANES), (pz1, None))
         v = jnp.concatenate([v[:ry1], v[ry1:]], axis=1)

time: 64.6 us -> 53.5 us (0.83)
  the two profiles are of different devices: /device:TPU:0 before, /device:TPU:12 now
where the time goes in v1:
time: 53.5 us; the launch traced here: 53.3 us
  Pallas kernels  51 us (95%)
  local copies, waits for them, and re-layouts  2.31 us (4%)
    pallas_call x1, Pallas kernels, per_device(): pl.pallas_call(functools.partial(kernel, counts, dims), out_shape=jax.Sha...  51 us
    unnamed x1, local copies, waits for them, and re-layouts  2.31 us

profile of v1, /device:TPU:12, one launch (start us, length us, event | category | flops | bytes accessed | tf_op | source)
XLA Modules:
  0.0 53.3 jit_solution(3163553780620655580)
XLA Ops:
  0.0 51.0 %shard_map.28 = f32[32,64,128]{2,1,0:T(8,128)} custom-call(f32[5,3,17]{2,1,0:T(4,128)} %taps.1, f32[32,64,128]{2,1,0:T(8,128)} %x_ref.1), custom_call_target="tpu_custom_call" | custom-call | tf_op jit(solution)/shard_map/pallas_call | solution.py:545
  51.0 2.3 %copy.4 = f32[32,64,128]{2,1,0:T(8,128)} copy(f32[32,64,128]{2,1,0:T(8,128)} %shard_map.28) | data formatting | bytes 2097152

commit v2 on v1

v2 whole, which is shorter than its diff:
```python
import functools

import jax
import jax.numpy as jnp
from jax import lax
from jax.experimental import pallas as pl
from jax.experimental.pallas import tpu as pltpu
from jax.sharding import PartitionSpec as P

F32, BF16 = jnp.float32, jnp.bfloat16
LANES = 128
U0, U1, U2, U3 = 4, 4, 4, 5
AXES = ("gx", "gy", "gz")
ODD = (-0.0625, 0.5625, 0.5625, -0.0625)
SIDES = tuple((a, b) for a in (-1, 0, 1) for b in (-1, 0, 1) if (a, b) != (0, 0))


def split(v):
    hi = v.astype(BF16)
    return hi, (v - hi.astype(F32)).astype(BF16)


def mm(a, b):
    return jnp.dot(a, b, preferred_element_type=F32)


def exact(a, b):
    return jnp.dot(a, b, preferred_element_type=F32, precision=lax.Precision.HIGHEST)


def dot_right(v, w):
    hi, lo = split(v)
    out = mm(hi, w[0][...]) + mm(lo, w[0][...])
    return out if w[1] is None else out + mm(hi, w[1][...])


def dot_left(w_ref, v, terms):
    hi, lo = split(v)
    return mm(w_ref[...], jnp.concatenate([hi, lo, hi][:terms], axis=0))


def grids(rows, cols):
    return (
        lax.broadcasted_iota(jnp.int32, (rows, cols), 0),
        lax.broadcasted_iota(jnp.int32, (rows, cols), 1),
    )


def pick(taps, level, axis, diff, ok):
    out = jnp.zeros(diff.shape, F32)
    for t in range(17):
        out = jnp.where(diff == t, taps[level, axis, t], out)
    return jnp.where(ok, out, 0.0)


def cubic(diff, ok):
    d = jnp.abs(diff)
    out = jnp.where(d == 0, 1.0, jnp.where(d == 1, 0.5625, jnp.where(d == 3, -0.0625, 0.0)))
    return jnp.where(ok, out, 0.0).astype(F32)


def up(n, m):
    return -(-n // m) * m


def inside(v, n):
    return (v >= 0) & (v < n)


def kernel(counts, dims, taps, x_ref, out_ref, e0, l0, r0, y0, y1, t1, t1l, t1r, e1, sw, f1, h1, h1l, h1r, d1, pr,
           ua, am, v2, v2l, v2r, pq, yu, yd, xg, g2, u2, y2,
           w0h, w0l, m0, w1h, w1l, m1, w2h, w2l, m2, c2, pz2, py2, py1, my2, wz2, ss, rs, sg, rg):
    nx, ny, nz = counts
    bx, by, bz = dims
    here = tuple(lax.axis_index(a) for a in AXES)
    gx, gy, gz = here
    cx, cy, cz = bx // 2, by // 2, bz // 2
    fx, fy, fz = bx // 4, by // 4, bz // 4
    half1 = cx // 2
    per = LANES // fz
    np2 = fx // per

    def there(dx, dy, dz):
        return inside(gx + dx, nx) & inside(gy + dy, ny) & inside(gz + dz, nz)

    partners = []
    for dim, n in enumerate(counts):
        for d in range(1, n):
            for sgn in (-d, d):
                partners.append(tuple(sgn if k == dim else 0 for k in range(3)))
    barrier = pltpu.get_barrier_semaphore()
    total = jnp.int32(0)
    for p in partners:
        ok = there(*p)
        total = total + ok.astype(jnp.int32)

        @pl.when(ok)
        def _(p=p):
            pl.semaphore_signal(
                barrier, inc=1, device_id=(gx + p[0], gy + p[1], gz + p[2]),
                device_id_type=pl.DeviceIdType.MESH,
            )

    def clear(ref, d, *at):
        @pl.when(jnp.logical_not(there(*d)))
        def _():
            view = ref.at[at]
            view[...] = jnp.zeros(view.shape, F32)

    every = slice(None)
    clear(e0, (0, -1, 0), every, pl.ds(0, 8))
    clear(e0, (0, 1, 0), every, pl.ds(8 + by, 8))
    clear(y0, (-1, 0, 0), pl.ds(0, 8))
    clear(y0, (1, 0, 0), pl.ds(8 + bx, 8))
    clear(t1l, (-1, 0, 0), every)
    clear(t1r, (1, 0, 0), every)
    clear(f1, (0, -1, 0), every, pl.ds(0, 16))
    clear(f1, (0, 1, 0), every, pl.ds(16 + cy, 16))
    clear(yu, (0, -1, 0), every)
    clear(yd, (0, 1, 0), every)
    for ref in (ua, y1):
        ref[pl.ds(0, 8)] = jnp.zeros((8,) + ref.shape[1:], F32)
        ref[pl.ds(8 + bx, 8)] = jnp.zeros((8,) + ref.shape[1:], F32)
    am[pl.ds(0, 6)] = jnp.zeros((6,) + am.shape[1:], F32)
    am[pl.ds(cx + 9, 6)] = jnp.zeros((6,) + am.shape[1:], F32)
    pl.semaphore_wait(barrier, total)

    count = [0]

    def remote(src, dst, d):
        k = count[0]
        count[0] += 1
        copy = pltpu.make_async_remote_copy(
            src_ref=src, dst_ref=dst, send_sem=ss.at[k], recv_sem=rs.at[k],
            device_id=(gx + d[0], gy + d[1], gz + d[2]), device_id_type=pl.DeviceIdType.MESH,
        )
        return there(*d), there(-d[0], -d[1], -d[2]), copy

    def start(copies):
        for to, _, copy in copies:
            pl.when(to)(copy.start)

    def arrive(copies):
        for _, fro, copy in copies:
            pl.when(fro)(copy.wait_recv)

    def left_over(copies):
        for to, _, copy in copies:
            pl.when(to)(copy.wait_send)

    right, left, ahead, behind, above, below = (
        (1, 0, 0), (-1, 0, 0), (0, 1, 0), (0, -1, 0), (0, 0, 1), (0, 0, -1)
    )
    own_y = pl.ds(8, by)
    ya = [
        remote(x_ref.at[:, pl.ds(by - 8, 8)], e0.at[:, pl.ds(0, 8)], ahead),
        remote(x_ref.at[:, pl.ds(0, 8)], e0.at[:, pl.ds(8 + by, 8)], behind),
    ]
    za = [remote(x_ref, l0.at[:, own_y], above), remote(x_ref, r0.at[:, own_y], below)]
    zf = [
        remote(e0.at[:, pl.ds(k, 8)], ref.at[:, pl.ds(k, 8)], d)
        for k in (0, 8 + by) for ref, d in ((l0, above), (r0, below))
    ]
    z2 = [remote(v2, v2l, above), remote(v2, v2r, below)]
    yp = [
        remote(pq.at[:, pl.ds(fy, 8)], yu, ahead),
        remote(pq.at[:, pl.ds(fy + 8, 8)], yd, behind),
    ]
    xa = [
        [
            remote(y0.at[pl.ds(bx + k, 2)], y0.at[pl.ds(k, 2)], right),
            remote(y0.at[pl.ds(8 + k, 2)], y0.at[pl.ds(8 + bx + k, 2)], left),
        ]
        for k in range(0, 8, 2)
    ]
    xb = [remote(t1.at[pl.ds(half1 - 4, 6)], t1l, right), remote(t1.at[pl.ds(0, 6)], t1r, left)]
    yb = [
        remote(f1.at[:, pl.ds(cy, 16)], f1.at[:, pl.ds(0, 16)], ahead),
        remote(f1.at[:, pl.ds(16, 16)], f1.at[:, pl.ds(16 + cy, 16)], behind),
    ]
    zb = [remote(h1, h1l, above), remote(h1, h1r, below)]
    start(ya)
    start(za)

    def put(h, l, v):
        hi, lo = split(v)
        h[...] = hi
        if l is not None:
            l[...] = lo

    def stack(ref, v, terms):
        hi, lo = split(v)
        ref[...] = jnp.concatenate([hi, hi, lo][:terms], axis=1)

    def twice(pos, at, base, n):
        out = jnp.zeros(pos.shape, F32)
        for k, w in ((-3, -0.0625), (-1, 0.5625), (0, 1.0), (1, 0.5625), (3, -0.0625)):
            m = 2 * at + k
            out = out + w * cubic(pos - 2 * m, inside(base + m, n))
        return out

    def restrict_x(ref, at):
        return (
            ref[at] + 0.5625 * (ref[at - 1] + ref[at + 1]) - 0.0625 * (ref[at - 3] + ref[at + 3])
        )

    lane = lax.broadcasted_iota(jnp.int32, (1, LANES), 1)
    has_r, has_l = there(*above), there(*below)
    mask_r, mask_l = (lane < LANES // 2) & has_r, (lane >= LANES // 2) & has_l
    rows2 = fy + 16
    i, j = grids(rows2, by)
    stack(my2, twice(j, jnp.where(i < fy + 8, i, i - rows2), gy * cy, ny * cy), 2)
    i, j = grids(2 * bz, LANES)
    pos = jnp.where(i < bz + bz // 2, i, i - 2 * bz)
    put(wz2, None, jnp.where(j < fz, twice(pos, j, gz * cz, nz * cz), 0.0))

    @pl.loop(0, bx // 2, unroll=4)
    def _(c):
        o = dot_left(my2, jnp.concatenate([x_ref[2 * c], x_ref[2 * c + 1]], axis=1), 2)
        ua[8 + 2 * c] = o[:, :LANES]
        ua[9 + 2 * c] = o[:, LANES:]

    for m in range(-1, cx + 2):
        am[m + 7] = restrict_x(ua, 8 + 2 * m) * inside(gx * cx + m, nx * cx).astype(F32)
    for e in range(fx + 5):
        v2[e] = restrict_x(am, 3 + 2 * e)
    start(z2)

    e0[:, own_y, :] = x_ref[...]
    i, j = grids(2 * bz, bz)
    pos = jnp.where(i < bz + bz // 2, i, i - 2 * bz)
    k0 = pick(taps, 0, 2, pos - j + 8, inside(pos, bz + 8) | inside(pos + 8, 8))
    rz = cubic(pos - 2 * j, j < cz)
    put(w0h, w0l, jnp.concatenate([k0, rz], axis=1))
    i, j = grids(by + cy, by + 16)
    stack(m0, jnp.where(i < by, pick(taps, 0, 1, j - i, i < by), cubic(j - 8 - 2 * (i - by), i >= by)), 3)

    arrive(z2)
    parts = []
    for e in range(fx + 5):
        other = jnp.where(mask_r, v2r[e], jnp.where(mask_l, v2l[e], 0.0))
        parts.append(jnp.concatenate([v2[e], other], axis=1))
    v = dot_right(jnp.concatenate(parts, axis=0), (wz2, None))
    for g in range(np2 + 2):
        acc = None
        for s in range(per):
            e = per * (g - 1) + s + 2
            if 0 <= e < fx + 5:
                w = v[e * rows2:(e + 1) * rows2]
                w = pltpu.roll(w, fz * s, 1) if s else w
                acc = w if acc is None else acc + w
        pq[g] = acc
    start(yp)

    i, j = grids(2 * cz, LANES)
    pos = jnp.where(i < cz + cz // 2, i, i - 2 * cz)
    kk = j - 2
    top = cz + 4
    ok = (j < top) & inside(gz * cz + kk, nz * cz)
    k1 = pick(taps, 1, 2, pos - kk + 8, ok)
    i, j = grids(LANES, bz)
    fine_z = cubic(j - 2 * (i - 2), i < top)
    put(w1h, w1l, exact(k1, fine_z))
    ry1 = up(cy + 4, 8)
    i, j = grids(ry1, cy + 32)
    ok = (i < cy + 4) & inside(gy * cy + i - 2, ny * cy)
    stack(m1, pick(taps, 1, 1, j - 16 - (i - 2) + 8, ok), 3)
    i, j = grids(by, up(ry1, 16))
    stack(py1, cubic(i - 2 * (j - 2), j < cy + 4), 2)

    def plain(axis, level, n, pad, turned):
        i, j = grids(pad, pad)
        d = (i - j if turned else j - i) + 8
        return pick(taps, level, axis, d, (i < n) & (j < n))

    def rest(n, pad, big, turned_r):
        i, j = grids(*((big, pad) if turned_r else (pad, big)))
        c, f = (j, i) if turned_r else (i, j)
        return cubic(f - 2 * c, (c < n) & (f < 2 * n))

    def operators(axis, n2, first, rows, count):
        n3, n4 = n2 // 2, n2 // 4
        q = up(n2, LANES)
        i, j = grids(rows, q)
        g = first + i
        ok = (i < count) & inside(g, n2)
        one = pick(taps, 2, axis, j - g + 8, ok & (j < n2))
        pr = cubic(g - 2 * j, ok & (j < n3))
        r23, r34 = rest(n3, q, q, False), rest(n4, q, q, False)
        p34 = rest(n4, q, q, True)
        two = exact(exact(pr, plain(axis, 3, n3, q, False)), r23)
        three = exact(exact(exact(exact(pr, p34), plain(axis, 4, n4, q, False)), r34), r23)
        return one, two, three

    n2x, n2y, n2z = nx * fx, ny * fy, nz * fz
    ez, ey, ex = fz + 5, fy + 5, fx + 5
    tz = 40
    ops = operators(2, n2z, gz * fz - 2, tz, ez)
    cols = jnp.concatenate(list(ops) + [jnp.zeros((LANES - 3 * tz, ops[0].shape[1]), F32)], axis=0)
    put(w2h, w2l, cols.T)
    ty = up(ey, 8)
    ops = operators(1, n2y, gy * fy - 2, ty, ey)
    stack(m2, jnp.concatenate(list(ops), axis=0)[:, :n2y], 3)
    tx = up(ex, 8)
    ops = operators(0, n2x, gx * fx - 2, tx, ex)
    tall = [o.T for o in ops]
    for r in range(ex):
        a, b, c = (o[:n2x, r:r + 1] for o in tall)
        c2[r] = jnp.where(lane < tz, a, jnp.where(lane < 2 * tz, b, c))
    i, j = grids(LANES, LANES)
    src = i - jnp.where(i < tz, 0, jnp.where(i < 2 * tz, tz, 2 * tz)) - 2
    e1_z = cubic((j - 2) - 2 * src, (i < 3 * tz) & (src < fz + 3) & (j < top) & inside(gz * cz + j - 2, nz * cz))
    put(pz2, None, exact(e1_z, fine_z))
    i, j = grids(ry1, up(ty, 16))
    stack(py2, cubic((i - 2) - 2 * (j - 2), (j < ey) & (i < cy + 4) & inside(gy * cy + i - 2, ny * cy)), 2)
    arrive(ya)
    start(zf)
    arrive(za)
    arrive(yp)
    own = [pq[:, pl.ds(0, 8)] + yu[...]]
    if fy > 16:
        own.append(pq[:, pl.ds(8, fy - 16)])
    own.append(pq[:, pl.ds(fy - 8, 8)] + yd[...])
    xg[gx] = jnp.concatenate(own, axis=1)
    def spread(dim, n, ref, k0):
        out = []
        for m, d in enumerate([d for d in range(-(n - 1), n) if d]):
            dev = tuple(here[k] + (d if k == dim else 0) for k in range(3))
            copy = pltpu.make_async_remote_copy(
                src_ref=ref(here[dim]), dst_ref=ref(here[dim]),
                send_sem=sg.at[dim, m], recv_sem=rg.at[dim, m],
                device_id=dev, device_id_type=pl.DeviceIdType.MESH,
            )
            land = pltpu.make_async_remote_copy(
                src_ref=ref(here[dim]), dst_ref=ref(here[dim] - d),
                send_sem=sg.at[dim, m], recv_sem=rg.at[dim, m],
                device_id=dev, device_id_type=pl.DeviceIdType.MESH,
            )
            to = inside(here[dim] + d, n)
            fro = inside(here[dim] - d, n)
            out.append((to, fro, copy, land))
        return out

    def begin(copies):
        for to, _, copy, _ in copies:
            pl.when(to)(copy.start)

    def landed(copies):
        for _, fro, _, land in copies:
            pl.when(fro)(land.wait_recv)

    ca = spread(0, nx, lambda k: xg.at[k], 0)
    begin(ca)
    arrive(zf)

    wide = by + 16
    step0 = 4

    def level0(c):
        at = pl.ds(c * step0, step0)
        own = e0[at].reshape(step0 * wide, LANES)
        other = jnp.where(
            mask_r, r0[at].reshape(step0 * wide, LANES),
            jnp.where(mask_l, l0[at].reshape(step0 * wide, LANES), 0.0),
        )
        v = dot_right(jnp.concatenate([own, other], axis=1), (w0h, w0l))
        for k in range(step0):
            o = dot_left(m0, v[k * wide:(k + 1) * wide], 3)
            y0[8 + c * step0 + k] = o[:by, :LANES]
            y1[8 + c * step0 + k] = o[by:, LANES:]

    edge = 8 // step0
    for c in range(edge):
        level0(c)
        level0(bx // step0 - edge + c)
    start(xa[0])
    pl.loop(edge, bx // step0 - edge, unroll=True)(level0)

    landed(ca)
    for m in range(np2 * nx):
        acc = None
        for b in range(nx):
            k = m - np2 * b + 1
            if 0 <= k < np2 + 2:
                acc = xg[b, k] if acc is None else acc + xg[b, k]
        g2[gz, gy, m] = acc
    cb = spread(1, ny, lambda k: g2.at[gz, k], 0)
    begin(cb)

    for p in range(half1 + 2):
        a = restrict_x(y1, 4 + 4 * p)
        b = restrict_x(y1, 6 + 4 * p)
        t1[p] = jnp.where(lane < cz, a, pltpu.roll(b, cz, 1))
    start(xb)
    for k in range(1, 4):
        start(xa[k])

    def conv0(p):
        acc = taps[0, 0, 0] * y0[p]
        for t in range(1, 17):
            acc = acc + taps[0, 0, t] * y0[p + t]
        out_ref[p] = acc

    pl.loop(8, bx - 8)(conv0)

    arrive(xb)
    n1 = half1 + 10
    to_l, to_r = there(*left).astype(F32), there(*right).astype(F32)
    for k in range(n1):
        if k < 4:
            v = t1l[k]
        elif k < 6:
            v = t1l[k] + (t1[k - 4] * to_l if k == 4 else t1[k - 4])
        elif k < half1 + 4:
            v = t1[k - 4]
        elif k < half1 + 6:
            v = t1r[k - half1 - 4] + (t1[k - 4] * to_r if k == half1 + 5 else t1[k - 4])
        else:
            v = t1r[k - half1 - 4]
        e1[k] = v
        back = pltpu.roll(v, cz, 1)
        if k:
            sw[k - 1] = jnp.where(lane < cz, last, back)
        last = back

    @pl.loop(0, half1 + 2)
    def _(q):
        acc = taps[1, 0, 0] * e1[q]
        for t in range(1, 17):
            acc = acc + taps[1, 0, t] * (sw[q + (t - 1) // 2] if t % 2 else e1[q + t // 2])
        f1[q, pl.ds(16, cy), :] = acc

    start(yb)
    landed(cb)
    cc = spread(2, nz, lambda k: g2.at[k], 0)
    begin(cc)
    arrive(yb)
    for q in range(0, half1 + 2, 2):
        o = dot_left(m1, jnp.concatenate([f1[q], f1[q + 1]], axis=1), 3)
        h1[q] = o[:, :LANES]
        h1[q + 1] = o[:, LANES:]
    start(zb)
    landed(cc)
    seen = lambda r: inside(gx * cx + r - 2, nx * cx).astype(F32)
    tiles = u2.shape[0]

    @pl.loop(0, nx * np2)
    def _(p):
        for b in range(ny):
            for k in range(per):
                for t in range(tiles):
                    acc = jnp.zeros((fy, LANES), F32)
                    for s in range(t * per, min(nz, (t + 1) * per)):
                        v = g2[s, b, p]
                        sh = (fz * (s - t * per - k)) % LANES
                        v = pltpu.roll(v, sh, 1) if sh else v
                        lo = fz * (s - t * per)
                        acc = jnp.where((lane >= lo) & (lane < lo + fz), v, acc)
                    u2[t, p * per + k, pl.ds(b * fy, fy), :] = acc

    step2 = 2

    @pl.loop(0, n2x // step2, unroll=U2)
    def _(c):
        at = pl.ds(c * step2, step2)
        v = jnp.concatenate([u2[t, at].reshape(step2 * n2y, LANES) for t in range(tiles)], axis=1)
        v = dot_right(v, (w2h, w2l))
        v = jnp.concatenate([v[k * n2y:(k + 1) * n2y] for k in range(step2)], axis=1)
        o = dot_left(m2, v, 3)
        for k in range(step2):
            w = o[:, k * LANES:(k + 1) * LANES]
            y2[c * step2 + k] = jnp.where(
                lane < tz, w[:ty], jnp.where(lane < 2 * tz, w[ty:2 * ty], w[2 * ty:])
            )

    parts = []
    for r in range(ex):
        acc = c2[r, pl.ds(0, 1)] * y2[0]
        for q in range(1, n2x):
            acc = acc + c2[r, pl.ds(q, 1)] * y2[q]
        parts.append(acc)
    v = dot_right(jnp.concatenate(parts, axis=0), (pz2, None))
    fill = up(ty, 16) - ty
    pro = []
    for r in range(ex):
        w = v[r * ty:(r + 1) * ty]
        if fill:
            w = jnp.concatenate([w, jnp.zeros((fill, LANES), F32)], axis=0)
        pro.append(dot_left(py2, w, 2))
    arrive(zb)
    near = lax.rem(lane, cz) < cz // 2
    step1 = 5 if (half1 + 2) % 5 == 0 else 1
    for c in range(0, half1 + 2, step1):
        parts = []
        for q in range(c, c + step1):
            own = h1[q]
            other = jnp.where(near & has_r, h1r[q], jnp.where(jnp.logical_not(near) & has_l, h1l[q], 0.0))
            parts.append(jnp.where(lane < cz, own, pltpu.roll(other, cz, 1)))
            parts.append(jnp.where(lane < cz, pltpu.roll(own, cz, 1), other))
        v = dot_right(jnp.concatenate(parts, axis=0), (w1h, w1l))
        for k in range(2 * step1):
            d1[2 * c + k] = v[k * ry1:(k + 1) * ry1]
    for p in range(cx + 4):
        m = (p - 2) // 2 + 2
        if p % 2 == 0:
            w = pro[m]
        else:
            w = 0.5625 * (pro[m] + pro[m + 1]) - 0.0625 * (pro[m - 1] + pro[m + 2])
        d1[p] = (d1[p] + w) * seen(p)

    fill1 = up(ry1, 16) - ry1

    @pl.loop(0, (cx + 4) // 2, unroll=5)
    def _(c):
        v = jnp.concatenate([d1[2 * c], d1[2 * c + 1]], axis=1)
        if fill1:
            v = jnp.concatenate([v, jnp.zeros((fill1, 2 * LANES), F32)], axis=0)
        o = dot_left(py1, v, 2)
        pr[2 * c] = o[:, :LANES]
        pr[2 * c + 1] = o[:, LANES:]

    for group in xa:
        arrive(group)
    pl.loop(0, 8)(conv0)
    pl.loop(bx - 8, bx)(conv0)

    @pl.loop(0, cx)
    def _(m):
        at = m + 2
        out_ref[2 * m] = out_ref[2 * m] + pr[at]
        out_ref[2 * m + 1] = out_ref[2 * m + 1] + (
            0.5625 * (pr[at] + pr[at + 1]) - 0.0625 * (pr[at - 1] + pr[at + 2])
        )

    for group in (ya, za, zf, z2, yp, *xa, xb, yb, zb):
        left_over(group)
    for group in (ca, cb, cc):
        for to, _, copy, _ in group:
            pl.when(to)(copy.wait_send)


def per_device(counts, charges, kernel_taps):
    nx, ny, nz = counts
    bx, by, bz = dims = charges.shape
    assert bz == LANES
    cx, cy, cz = bx // 2, by // 2, bz // 2
    fx, fy, fz = bx // 4, by // 4, bz // 4
    n2x, n2y, n2z = nx * fx, ny * fy, nz * fz
    np2 = fx // (LANES // fz)
    half1 = cx // 2
    ry1 = up(cy + 4, 8)
    ty = up(fy + 5, 8)
    tiles = up(n2z, LANES) // LANES
    V = pltpu.VMEM
    ext0 = (bx, by + 16, LANES)
    wide = max(nx, ny, nz) * 2
    dma = pltpu.SemaphoreType.DMA
    row = lambda n, r: V((n, r, LANES), F32)
    scratch = [
        V(ext0, F32), V(ext0, F32), V(ext0, F32),
        row(bx + 16, by), row(bx + 16, cy),
        row(half1 + 2, cy), row(6, cy), row(6, cy), row(half1 + 10, cy), row(half1 + 9, cy),
        row(half1 + 2, cy + 32), row(half1 + 2, ry1), row(half1 + 2, ry1), row(half1 + 2, ry1),
        row(cx + 4, ry1), row(cx + 4, by),
        row(bx + 16, fy + 16), row(cx + 15, fy + 16),
        row(fx + 5, fy + 16), row(fx + 5, fy + 16), row(fx + 5, fy + 16),
        row(np2 + 2, fy + 16), row(np2 + 2, 8), row(np2 + 2, 8),
        V((nx, np2 + 2, fy, LANES), F32),
        V((nz, ny, nx * np2, fy, LANES), F32),
        V((tiles, n2x, n2y, LANES), F32),
        row(n2x, ty),
        V((2 * bz, bz + LANES), BF16), V((2 * bz, bz + LANES), BF16),
        V((by + cy, 3 * (by + 16)), BF16),
        V((2 * cz, bz), BF16), V((2 * cz, bz), BF16),
        V((ry1, 3 * (cy + 32)), BF16),
        V((tiles * LANES, LANES), BF16), V((tiles * LANES, LANES), BF16),
        V((3 * ty, 3 * n2y), BF16),
        row(fx + 5, n2x),
        V((LANES, bz), BF16), V((ry1, 2 * up(ty, 16)), BF16),
        V((by, 2 * up(ry1, 16)), BF16),
        V((fy + 16, 2 * by), BF16), V((2 * bz, LANES), BF16),
        dma((32,)), dma((32,)), dma((3, wide)), dma((3, wide)),
    ]
    return pl.pallas_call(
        functools.partial(kernel, counts, dims),
        out_shape=jax.ShapeDtypeStruct(dims, F32),
        in_specs=[pl.BlockSpec(memory_space=pltpu.SMEM), pl.BlockSpec(memory_space=pltpu.VMEM)],
        out_specs=pl.BlockSpec(memory_space=pltpu.VMEM),
        scratch_shapes=scratch,
        compiler_params=pltpu.CompilerParams(
            collective_id=0, has_side_effects=True, vmem_limit_bytes=28 * 2**20
        ),
    )(kernel_taps, charges)


def solution(mesh):
    counts = tuple(mesh.shape[a] for a in AXES)
    return jax.shard_map(
        functools.partial(per_device, counts), mesh=mesh,
        in_specs=(P("gx", "gy", "gz"), P()), out_specs=P("gx", "gy", "gz"), check_vma=False,
    )
```

time: 53.5 us -> 39.5 us (0.74)
  the two profiles are of different devices: /device:TPU:12 before, /device:TPU:0 now
where the time goes in v2:
time: 39.5 us; the launch traced here: 39.3 us
  Pallas kernels  36.4 us (92%)
  local copies, waits for them, and re-layouts  2.9 us (7%)
    pallas_call x1, Pallas kernels, per_device(): pl.pallas_call(functools.partial(kernel, counts, dims), out_shape=jax.Sha...  36.4 us
    unnamed x5, local copies, waits for them, and re-layouts  2.9 us

profile of v2, /device:TPU:0, one launch (start us, length us, event | category | flops | bytes accessed | tf_op | source)
XLA Modules:
  0.0 39.3 jit_solution(3419084112834583314)
XLA Ops:
  0.0 0.0 copy-start
  0.0 1.2 %copy-done = f32[32,64,128]{2,1,0:T(8,128)S(1)} copy-done((f32[32,64,128]{2,1,0:T(8,128)S(1)}, f32[32,64,128]{2,1,0:T(8,128)}, u32[]{:S(2)}) %copy-start) | copy-done | bytes 1048600
  1.2 0.0 copy-start.1
  1.2 0.7 %copy-done.1 = f32[5,3,17]{2,1,0:T(4,128)S(1)} copy-done((f32[5,3,17]{2,1,0:T(4,128)S(1)}, f32[5,3,17]{2,1,0:T(4,128)}, u32[]{:S(2)}) %copy-start.1) | copy-done | bytes 1044
  1.9 36.4 %shard_map.28 = f32[32,64,128]{2,1,0:T(8,128)S(1)} custom-call(f32[5,3,17]{2,1,0:T(4,128)S(1)} %copy-done.1, f32[32,64,128]{2,1,0:T(8,128)S(1)} %copy-done), custom_call_target="tpu_custom_call" | custom-call | tf_op jit(solution)/shard_map/pallas_call | solution.py:584
  38.4 1.0 %copy.4 = f32[32,64,128]{2,1,0:T(8,128)} copy(f32[32,64,128]{2,1,0:T(8,128)S(1)} %shard_map.28) | data formatting | bytes 2097152
Async XLA Ops:
  0.0 1.2 %copy-start = (f32[32,64,128]{2,1,0:T(8,128)S(1)}, f32[32,64,128]{2,1,0:T(8,128)}, u32[]{:S(2)}) copy-start(f32[32,64,128]{2,1,0:T(8,128)} %x_ref.1) | copy-start | bytes 3145732
  1.2 0.7 %copy-start.1 = (f32[5,3,17]{2,1,0:T(4,128)S(1)}, f32[5,3,17]{2,1,0:T(4,128)}, u32[]{:S(2)}) copy-start(f32[5,3,17]{2,1,0:T(4,128)} %taps.1) | copy-start | bytes 3064

commit v3 on v2

--- a/solution.py
+++ b/solution.py
@@ -67,12 +67,18 @@
     return (v >= 0) & (v < n)
 
 
-def kernel(counts, dims, taps, x_ref, out_ref, e0, l0, r0, y0, y1, t1, t1l, t1r, e1, sw, f1, h1, h1l, h1r, d1, pr,
-           ua, am, v2, v2l, v2r, pq, yu, yd, xg, g2, u2, y2,
-           w0h, w0l, m0, w1h, w1l, m1, w2h, w2l, m2, c2, pz2, py2, py1, my2, wz2, ss, rs, sg, rg):
+def kernel(counts, dims, taps_hbm, x_hbm, out_ref, taps, x_ref, l0, r0, hy, hl, hr, zh, zl, y0, y1, t1, t1l, t1r, e1, sw, f1, h1, h1l, h1r, d1, pr,
+           ua, am, v2, v2l, v2r, pq, yu, yd, xg, g2, z2h, z2l, y2,
+           w0h, w0l, m0, w1h, w1l, m1, w2h, w2l, m2, c2, pz2, py2, py1, my2, wz2, own_sem, ss, rs, sg, rg):
     nx, ny, nz = counts
     bx, by, bz = dims
     here = tuple(lax.axis_index(a) for a in AXES)
+    loads = [
+        pltpu.make_async_copy(x_hbm, x_ref, own_sem.at[0]),
+        pltpu.make_async_copy(taps_hbm, taps, own_sem.at[1]),
+    ]
+    for load in loads:
+        load.start()
     gx, gy, gz = here
     cx, cy, cz = bx // 2, by // 2, bz // 2
     fx, fy, fz = bx // 4, by // 4, bz // 4
@@ -108,8 +114,8 @@
             view[...] = jnp.zeros(view.shape, F32)
 
     every = slice(None)
-    clear(e0, (0, -1, 0), every, pl.ds(0, 8))
-    clear(e0, (0, 1, 0), every, pl.ds(8 + by, 8))
+    clear(hy, (0, -1, 0), every, pl.ds(0, 8))
+    clear(hy, (0, 1, 0), every, pl.ds(8, 8))
     clear(y0, (-1, 0, 0), pl.ds(0, 8))
     clear(y0, (1, 0, 0), pl.ds(8 + bx, 8))
     clear(t1l, (-1, 0, 0), every)
@@ -123,6 +129,8 @@
         ref[pl.ds(8 + bx, 8)] = jnp.zeros((8,) + ref.shape[1:], F32)
     am[pl.ds(0, 6)] = jnp.zeros((6,) + am.shape[1:], F32)
     am[pl.ds(cx + 9, 6)] = jnp.zeros((6,) + am.shape[1:], F32)
+    for load in loads:
+        load.wait()
     pl.semaphore_wait(barrier, total)
 
     count = [0]
@@ -151,16 +159,16 @@
     right, left, ahead, behind, above, below = (
         (1, 0, 0), (-1, 0, 0), (0, 1, 0), (0, -1, 0), (0, 0, 1), (0, 0, -1)
     )
-    own_y = pl.ds(8, by)
-    ya = [
-        remote(x_ref.at[:, pl.ds(by - 8, 8)], e0.at[:, pl.ds(0, 8)], ahead),
-        remote(x_ref.at[:, pl.ds(0, 8)], e0.at[:, pl.ds(8 + by, 8)], behind),
-    ]
-    za = [remote(x_ref, l0.at[:, own_y], above), remote(x_ref, r0.at[:, own_y], below)]
-    zf = [
-        remote(e0.at[:, pl.ds(k, 8)], ref.at[:, pl.ds(k, 8)], d)
-        for k in (0, 8 + by) for ref, d in ((l0, above), (r0, below))
-    ]
+    ends = (pl.ds(0, 8), pl.ds(bx - 8, 8)), (pl.ds(8, bx - 16),)
+    ya, zf = [], []
+    for xs in ends:
+        ya.append([
+            remote(x_ref.at[x, pl.ds(by - 8, 8)], hy.at[x, pl.ds(0, 8)], ahead) for x in xs
+        ] + [
+            remote(x_ref.at[x, pl.ds(0, 8)], hy.at[x, pl.ds(8, 8)], behind) for x in xs
+        ])
+        zf.append([remote(hy.at[x], hl.at[x], above) for x in xs] + [remote(hy.at[x], hr.at[x], below) for x in xs])
+    za = [remote(x_ref, l0, above), remote(x_ref, r0, below)]
     z2 = [remote(v2, v2l, above), remote(v2, v2r, below)]
     yp = [
         remote(pq.at[:, pl.ds(fy, 8)], yu, ahead),
@@ -168,10 +176,10 @@
     ]
     xa = [
         [
-            remote(y0.at[pl.ds(bx + k, 2)], y0.at[pl.ds(k, 2)], right),
-            remote(y0.at[pl.ds(8 + k, 2)], y0.at[pl.ds(8 + bx + k, 2)], left),
+            remote(y0.at[pl.ds(bx + k, n)], y0.at[pl.ds(k, n)], right),
+            remote(y0.at[pl.ds(8 + k, n)], y0.at[pl.ds(8 + bx + k, n)], left),
         ]
-        for k in range(0, 8, 2)
+        for k, n in ((0, 2), (2, 6))
     ]
     xb = [remote(t1.at[pl.ds(half1 - 4, 6)], t1l, right), remote(t1.at[pl.ds(0, 6)], t1r, left)]
     yb = [
@@ -179,8 +187,9 @@
         remote(f1.at[:, pl.ds(16, 16)], f1.at[:, pl.ds(16 + cy, 16)], behind),
     ]
     zb = [remote(h1, h1l, above), remote(h1, h1r, below)]
-    start(ya)
+    start(ya[0])
     start(za)
+    start(ya[1])
 
     def put(h, l, v):
         hi, lo = split(v)
@@ -226,15 +235,48 @@
         v2[e] = restrict_x(am, 3 + 2 * e)
     start(z2)
 
-    e0[:, own_y, :] = x_ref[...]
     i, j = grids(2 * bz, bz)
     pos = jnp.where(i < bz + bz // 2, i, i - 2 * bz)
     k0 = pick(taps, 0, 2, pos - j + 8, inside(pos, bz + 8) | inside(pos + 8, 8))
     rz = cubic(pos - 2 * j, j < cz)
     put(w0h, w0l, jnp.concatenate([k0, rz], axis=1))
     i, j = grids(by + cy, by + 16)
+    j = jnp.where(j < by, j + 8, jnp.where(j < by + 8, j - by, j))
     stack(m0, jnp.where(i < by, pick(taps, 0, 1, j - i, i < by), cubic(j - 8 - 2 * (i - by), i >= by)), 3)
 
+    step0 = 4
+
+    def across(own, lo, hi):
+        rows = own.shape[0] * own.shape[1]
+        other = jnp.where(
+            mask_r, hi.reshape(rows, LANES), jnp.where(mask_l, lo.reshape(rows, LANES), 0.0)
+        )
+        v = jnp.concatenate([own.reshape(rows, LANES), other], axis=1)
+        return split(dot_right(v, (w0h, w0l)))
+
+    def level0_own(c):
+        at = pl.ds(c * step0, step0)
+        hi, lo = across(x_ref[at], l0[at], r0[at])
+        zh[at, pl.ds(0, by), :] = hi.reshape(step0, by, 2 * LANES)
+        zl[at, pl.ds(0, by), :] = lo.reshape(step0, by, 2 * LANES)
+
+    def level0_halo(x, n):
+        at = pl.ds(x, n)
+        hi, lo = across(hy[at], hl[at], hr[at])
+        zh[at, pl.ds(by, 16), :] = hi.reshape(n, 16, 2 * LANES)
+        zl[at, pl.ds(by, 16), :] = lo.reshape(n, 16, 2 * LANES)
+
+    def level0(k):
+        hi = zh[k]
+        o = mm(m0[...], jnp.concatenate([hi, zl[k], hi], axis=0))
+        y0[8 + k] = o[:by, :LANES]
+        y1[8 + k] = o[by:, LANES:]
+
+    arrive(za)
+    edge = 8 // step0
+    for c in range(edge):
+        level0_own(c)
+        level0_own(bx // step0 - edge + c)
     arrive(z2)
     parts = []
     for e in range(fx + 5):
@@ -252,76 +294,17 @@
         pq[g] = acc
     start(yp)
 
-    i, j = grids(2 * cz, LANES)
-    pos = jnp.where(i < cz + cz // 2, i, i - 2 * cz)
-    kk = j - 2
-    top = cz + 4
-    ok = (j < top) & inside(gz * cz + kk, nz * cz)
-    k1 = pick(taps, 1, 2, pos - kk + 8, ok)
-    i, j = grids(LANES, bz)
-    fine_z = cubic(j - 2 * (i - 2), i < top)
-    put(w1h, w1l, exact(k1, fine_z))
-    ry1 = up(cy + 4, 8)
-    i, j = grids(ry1, cy + 32)
-    ok = (i < cy + 4) & inside(gy * cy + i - 2, ny * cy)
-    stack(m1, pick(taps, 1, 1, j - 16 - (i - 2) + 8, ok), 3)
-    i, j = grids(by, up(ry1, 16))
-    stack(py1, cubic(i - 2 * (j - 2), j < cy + 4), 2)
-
-    def plain(axis, level, n, pad, turned):
-        i, j = grids(pad, pad)
-        d = (i - j if turned else j - i) + 8
-        return pick(taps, level, axis, d, (i < n) & (j < n))
-
-    def rest(n, pad, big, turned_r):
-        i, j = grids(*((big, pad) if turned_r else (pad, big)))
-        c, f = (j, i) if turned_r else (i, j)
-        return cubic(f - 2 * c, (c < n) & (f < 2 * n))
-
-    def operators(axis, n2, first, rows, count):
-        n3, n4 = n2 // 2, n2 // 4
-        q = up(n2, LANES)
-        i, j = grids(rows, q)
-        g = first + i
-        ok = (i < count) & inside(g, n2)
-        one = pick(taps, 2, axis, j - g + 8, ok & (j < n2))
-        pr = cubic(g - 2 * j, ok & (j < n3))
-        r23, r34 = rest(n3, q, q, False), rest(n4, q, q, False)
-        p34 = rest(n4, q, q, True)
-        two = exact(exact(pr, plain(axis, 3, n3, q, False)), r23)
-        three = exact(exact(exact(exact(pr, p34), plain(axis, 4, n4, q, False)), r34), r23)
-        return one, two, three
-
-    n2x, n2y, n2z = nx * fx, ny * fy, nz * fz
-    ez, ey, ex = fz + 5, fy + 5, fx + 5
-    tz = 40
-    ops = operators(2, n2z, gz * fz - 2, tz, ez)
-    cols = jnp.concatenate(list(ops) + [jnp.zeros((LANES - 3 * tz, ops[0].shape[1]), F32)], axis=0)
-    put(w2h, w2l, cols.T)
-    ty = up(ey, 8)
-    ops = operators(1, n2y, gy * fy - 2, ty, ey)
-    stack(m2, jnp.concatenate(list(ops), axis=0)[:, :n2y], 3)
-    tx = up(ex, 8)
-    ops = operators(0, n2x, gx * fx - 2, tx, ex)
-    tall = [o.T for o in ops]
-    for r in range(ex):
-        a, b, c = (o[:n2x, r:r + 1] for o in tall)
-        c2[r] = jnp.where(lane < tz, a, jnp.where(lane < 2 * tz, b, c))
-    i, j = grids(LANES, LANES)
-    src = i - jnp.where(i < tz, 0, jnp.where(i < 2 * tz, tz, 2 * tz)) - 2
-    e1_z = cubic((j - 2) - 2 * src, (i < 3 * tz) & (src < fz + 3) & (j < top) & inside(gz * cz + j - 2, nz * cz))
-    put(pz2, None, exact(e1_z, fine_z))
-    i, j = grids(ry1, up(ty, 16))
-    stack(py2, cubic((i - 2) - 2 * (j - 2), (j < ey) & (i < cy + 4) & inside(gy * cy + i - 2, ny * cy)), 2)
-    arrive(ya)
-    start(zf)
-    arrive(za)
-    arrive(yp)
-    own = [pq[:, pl.ds(0, 8)] + yu[...]]
-    if fy > 16:
-        own.append(pq[:, pl.ds(8, fy - 16)])
-    own.append(pq[:, pl.ds(fy - 8, 8)] + yd[...])
-    xg[gx] = jnp.concatenate(own, axis=1)
+    arrive(ya[0])
+    start(zf[0])
+    pl.loop(edge, bx // step0 - edge, unroll=4)(level0_own)
+    arrive(ya[1])
+    start(zf[1])
+    arrive(zf[0])
+    level0_halo(0, 8)
+    level0_halo(bx - 8, 8)
+    for k in range(8):
+        level0(k)
+        level0(bx - 8 + k)
     def spread(dim, n, ref, k0):
         out = []
         for m, d in enumerate([d for d in range(-(n - 1), n) if d]):
@@ -349,32 +332,33 @@
         for _, fro, _, land in copies:
             pl.when(fro)(land.wait_recv)
 
+    arrive(yp)
+    own = [pq[:, pl.ds(0, 8)] + yu[...]]
+    if fy > 16:
+        own.append(pq[:, pl.ds(8, fy - 16)])
+    own.append(pq[:, pl.ds(fy - 8, 8)] + yd[...])
+    xg[gx] = jnp.concatenate(own, axis=1)
     ca = spread(0, nx, lambda k: xg.at[k], 0)
     begin(ca)
-    arrive(zf)
-
-    wide = by + 16
-    step0 = 4
-
-    def level0(c):
-        at = pl.ds(c * step0, step0)
-        own = e0[at].reshape(step0 * wide, LANES)
-        other = jnp.where(
-            mask_r, r0[at].reshape(step0 * wide, LANES),
-            jnp.where(mask_l, l0[at].reshape(step0 * wide, LANES), 0.0),
-        )
-        v = dot_right(jnp.concatenate([own, other], axis=1), (w0h, w0l))
-        for k in range(step0):
-            o = dot_left(m0, v[k * wide:(k + 1) * wide], 3)
-            y0[8 + c * step0 + k] = o[:by, :LANES]
-            y1[8 + c * step0 + k] = o[by:, LANES:]
-
-    edge = 8 // step0
-    for c in range(edge):
-        level0(c)
-        level0(bx // step0 - edge + c)
     start(xa[0])
-    pl.loop(edge, bx // step0 - edge, unroll=True)(level0)
+    arrive(zf[1])
+    level0_halo(8, bx - 16)
+    pl.loop(8, bx - 8, unroll=8)(level0)
+
+    for p in range(half1 + 2):
+        a = restrict_x(y1, 4 + 4 * p)
+        b = restrict_x(y1, 6 + 4 * p)
+        t1[p] = jnp.where(lane < cz, a, pltpu.roll(b, cz, 1))
+    start(xb)
+    start(xa[1])
+
+    def conv0(p):
+        acc = taps[0, 0, 0] * y0[p]
+        for t in range(1, 17):
+            acc = acc + taps[0, 0, t] * y0[p + t]
+        out_ref[p] = acc
+
+    pl.loop(8, bx - 8)(conv0)
 
     landed(ca)
     for m in range(np2 * nx):
@@ -387,22 +371,72 @@
     cb = spread(1, ny, lambda k: g2.at[gz, k], 0)
     begin(cb)
 
-    for p in range(half1 + 2):
-        a = restrict_x(y1, 4 + 4 * p)
-        b = restrict_x(y1, 6 + 4 * p)
-        t1[p] = jnp.where(lane < cz, a, pltpu.roll(b, cz, 1))
-    start(xb)
-    for k in range(1, 4):
-        start(xa[k])
-
-    def conv0(p):
-        acc = taps[0, 0, 0] * y0[p]
-        for t in range(1, 17):
-            acc = acc + taps[0, 0, t] * y0[p + t]
-        out_ref[p] = acc
-
-    pl.loop(8, bx - 8)(conv0)
-
+    i, j = grids(2 * cz, LANES)
+    pos = jnp.where(i < cz + cz // 2, i, i - 2 * cz)
+    kk = j - 2
+    top = cz + 4
+    ok = (j < top) & inside(gz * cz + kk, nz * cz)
+    k1 = pick(taps, 1, 2, pos - kk + 8, ok)
+    i, j = grids(LANES, bz)
+    fine_z = cubic(j - 2 * (i - 2), i < top)
+    put(w1h, w1l, exact(k1, fine_z))
+    ry1 = up(cy + 4, 8)
+    i, j = grids(ry1, cy + 32)
+    ok = (i < cy + 4) & inside(gy * cy + i - 2, ny * cy)
+    stack(m1, pick(taps, 1, 1, j - 16 - (i - 2) + 8, ok), 3)
+    i, j = grids(by, up(ry1, 16))
+    stack(py1, cubic(i - 2 * (j - 2), j < cy + 4), 2)
+
+    def plain(axis, level, n, pad, turned):
+        i, j = grids(pad, pad)
+        d = (i - j if turned else j - i) + 8
+        return pick(taps, level, axis, d, (i < n) & (j < n))
+
+    def rest(n, pad, big, turned_r):
+        i, j = grids(*((big, pad) if turned_r else (pad, big)))
+        c, f = (j, i) if turned_r else (i, j)
+        return cubic(f - 2 * c, (c < n) & (f < 2 * n))
+
+    def operators(axis, n2, first, rows, count):
+        n3, n4 = n2 // 2, n2 // 4
+        q = up(n2, LANES)
+        i, j = grids(rows, q)
+        g = first + i
+        ok = (i < count) & inside(g, n2)
+        one = pick(taps, 2, axis, j - g + 8, ok & (j < n2))
+        pr = cubic(g - 2 * j, ok & (j < n3))
+        r23, r34 = rest(n3, q, q, False), rest(n4, q, q, False)
+        p34 = rest(n4, q, q, True)
+        two = exact(exact(pr, plain(axis, 3, n3, q, False)), r23)
+        three = exact(exact(exact(exact(pr, p34), plain(axis, 4, n4, q, False)), r34), r23)
+        return one, two, three
+
+    n2x, n2y, n2z = nx * fx, ny * fy, nz * fz
+    ez, ey, ex = fz + 5, fy + 5, fx + 5
+    tz = 40
+    ops = operators(2, n2z, gz * fz - 2, tz, ez)
+    cols = jnp.concatenate(list(ops) + [jnp.zeros((LANES - 3 * tz, ops[0].shape[1]), F32)], axis=0)
+    hi, lo = split(cols.T)
+    for ref, v in ((w2h, hi), (w2l, lo)):
+        ref[...] = jnp.zeros(ref.shape, BF16)
+        for b in range(nz):
+            for k in range(per):
+                ref[pl.ds(b * LANES + k * fz, fz), pl.ds(k * LANES, LANES)] = v[b * fz:(b + 1) * fz]
+    ty = up(ey, 8)
+    ops = operators(1, n2y, gy * fy - 2, ty, ey)
+    stack(m2, jnp.concatenate(list(ops), axis=0)[:, :n2y], 3)
+    tx = up(ex, 8)
+    ops = operators(0, n2x, gx * fx - 2, tx, ex)
+    tall = [o.T for o in ops]
+    for r in range(ex):
+        a, b, c = (o[:n2x, r:r + 1] for o in tall)
+        c2[r] = jnp.where(lane < tz, a, jnp.where(lane < 2 * tz, b, c))
+    i, j = grids(LANES, LANES)
+    src = i - jnp.where(i < tz, 0, jnp.where(i < 2 * tz, tz, 2 * tz)) - 2
+    e1_z = cubic((j - 2) - 2 * src, (i < 3 * tz) & (src < fz + 3) & (j < top) & inside(gz * cz + j - 2, nz * cz))
+    put(pz2, None, exact(e1_z, fine_z))
+    i, j = grids(ry1, up(ty, 16))
+    stack(py2, cubic((i - 2) - 2 * (j - 2), (j < ey) & (i < cy + 4) & inside(gy * cy + i - 2, ny * cy)), 2)
     arrive(xb)
     n1 = half1 + 10
     to_l, to_r = there(*left).astype(F32), there(*right).astype(F32)
@@ -442,34 +476,23 @@
     start(zb)
     landed(cc)
     seen = lambda r: inside(gx * cx + r - 2, nx * cx).astype(F32)
-    tiles = u2.shape[0]
-
-    @pl.loop(0, nx * np2)
-    def _(p):
-        for b in range(ny):
-            for k in range(per):
-                for t in range(tiles):
-                    acc = jnp.zeros((fy, LANES), F32)
-                    for s in range(t * per, min(nz, (t + 1) * per)):
-                        v = g2[s, b, p]
-                        sh = (fz * (s - t * per - k)) % LANES
-                        v = pltpu.roll(v, sh, 1) if sh else v
-                        lo = fz * (s - t * per)
-                        acc = jnp.where((lane >= lo) & (lane < lo + fz), v, acc)
-                    u2[t, p * per + k, pl.ds(b * fy, fy), :] = acc
-
-    step2 = 2
-
-    @pl.loop(0, n2x // step2, unroll=U2)
-    def _(c):
-        at = pl.ds(c * step2, step2)
-        v = jnp.concatenate([u2[t, at].reshape(step2 * n2y, LANES) for t in range(tiles)], axis=1)
-        v = dot_right(v, (w2h, w2l))
-        v = jnp.concatenate([v[k * n2y:(k + 1) * n2y] for k in range(step2)], axis=1)
-        o = dot_left(m2, v, 3)
-        for k in range(step2):
+    batch = max(1, min(nx * np2, 256 // n2y))
+    for m in range(0, nx * np2, batch):
+        v = jnp.concatenate([
+            jnp.concatenate([g2[b, :, k].reshape(n2y, LANES) for b in range(nz)], axis=1)
+            for k in range(m, m + batch)
+        ], axis=0)
+        hi, lo = split(dot_right(v, (w2h, w2l)))
+        z2h[pl.ds(m, batch)] = hi.reshape(batch, n2y, per * LANES)
+        z2l[pl.ds(m, batch)] = lo.reshape(batch, n2y, per * LANES)
+
+    @pl.loop(0, nx * np2, unroll=4)
+    def _(m):
+        hi = z2h[m]
+        o = mm(m2[...], jnp.concatenate([hi, z2l[m], hi], axis=0))
+        for k in range(per):
             w = o[:, k * LANES:(k + 1) * LANES]
-            y2[c * step2 + k] = jnp.where(
+            y2[per * m + k] = jnp.where(
                 lane < tz, w[:ty], jnp.where(lane < 2 * tz, w[ty:2 * ty], w[2 * ty:])
             )
 
@@ -532,7 +555,7 @@
             0.5625 * (pr[at] + pr[at + 1]) - 0.0625 * (pr[at - 1] + pr[at + 2])
         )
 
-    for group in (ya, za, zf, z2, yp, *xa, xb, yb, zb):
+    for group in (*ya, za, *zf, z2, yp, *xa, xb, yb, zb):
         left_over(group)
     for group in (ca, cb, cc):
         for to, _, copy, _ in group:
@@ -546,18 +569,19 @@
     cx, cy, cz = bx // 2, by // 2, bz // 2
     fx, fy, fz = bx // 4, by // 4, bz // 4
     n2x, n2y, n2z = nx * fx, ny * fy, nz * fz
-    np2 = fx // (LANES // fz)
+    per = LANES // fz
+    np2 = fx // per
     half1 = cx // 2
     ry1 = up(cy + 4, 8)
     ty = up(fy + 5, 8)
-    tiles = up(n2z, LANES) // LANES
     V = pltpu.VMEM
-    ext0 = (bx, by + 16, LANES)
     wide = max(nx, ny, nz) * 2
     dma = pltpu.SemaphoreType.DMA
     row = lambda n, r: V((n, r, LANES), F32)
     scratch = [
-        V(ext0, F32), V(ext0, F32), V(ext0, F32),
+        pltpu.SMEM(kernel_taps.shape, F32), V(dims, F32),
+        row(bx, by), row(bx, by), row(bx, 16), row(bx, 16), row(bx, 16),
+        V((bx, by + 16, 2 * LANES), BF16), V((bx, by + 16, 2 * LANES), BF16),
         row(bx + 16, by), row(bx + 16, cy),
         row(half1 + 2, cy), row(6, cy), row(6, cy), row(half1 + 10, cy), row(half1 + 9, cy),
         row(half1 + 2, cy + 32), row(half1 + 2, ry1), row(half1 + 2, ry1), row(half1 + 2, ry1),
@@ -567,28 +591,28 @@
         row(np2 + 2, fy + 16), row(np2 + 2, 8), row(np2 + 2, 8),
         V((nx, np2 + 2, fy, LANES), F32),
         V((nz, ny, nx * np2, fy, LANES), F32),
-        V((tiles, n2x, n2y, LANES), F32),
+        V((nx * np2, n2y, per * LANES), BF16), V((nx * np2, n2y, per * LANES), BF16),
         row(n2x, ty),
         V((2 * bz, bz + LANES), BF16), V((2 * bz, bz + LANES), BF16),
         V((by + cy, 3 * (by + 16)), BF16),
         V((2 * cz, bz), BF16), V((2 * cz, bz), BF16),
         V((ry1, 3 * (cy + 32)), BF16),
-        V((tiles * LANES, LANES), BF16), V((tiles * LANES, LANES), BF16),
+        V((nz * LANES, per * LANES), BF16), V((nz * LANES, per * LANES), BF16),
         V((3 * ty, 3 * n2y), BF16),
         row(fx + 5, n2x),
         V((LANES, bz), BF16), V((ry1, 2 * up(ty, 16)), BF16),
         V((by, 2 * up(ry1, 16)), BF16),
         V((fy + 16, 2 * by), BF16), V((2 * bz, LANES), BF16),
-        dma((32,)), dma((32,)), dma((3, wide)), dma((3, wide)),
+        dma((2,)), dma((32,)), dma((32,)), dma((3, wide)), dma((3, wide)),
     ]
     return pl.pallas_call(
         functools.partial(kernel, counts, dims),
         out_shape=jax.ShapeDtypeStruct(dims, F32),
-        in_specs=[pl.BlockSpec(memory_space=pltpu.SMEM), pl.BlockSpec(memory_space=pltpu.VMEM)],
+        in_specs=[pl.BlockSpec(memory_space=pltpu.HBM)] * 2,
         out_specs=pl.BlockSpec(memory_space=pltpu.VMEM),
         scratch_shapes=scratch,
         compiler_params=pltpu.CompilerParams(
-            collective_id=0, has_side_effects=True, vmem_limit_bytes=28 * 2**20
+            collective_id=0, has_side_effects=True, vmem_limit_bytes=105 * 2**19
         ),
     )(kernel_taps, charges)
 

time: 39.5 us -> 33.6 us (0.85)
  Pallas kernels: 36.4 us -> 31.7 us
  local copies, waits for them, and re-layouts: 2.9 us -> 1.67 us
    pallas_call x1, Pallas kernels: 36.4 us -> 31.7 us  [per_device(): pl.pallas_call(functools.partial(kernel, counts, dims), out_shape=jax.Sha...]
    unnamed x5 -> x3, local copies, waits for them, and re-layouts: 2.9 us -> 1.67 us
where the time goes in v3:
time: 33.6 us; the launch traced here: 33.4 us
  Pallas kernels  31.7 us (94%)
  local copies, waits for them, and re-layouts  1.67 us (5%)
    pallas_call x1, Pallas kernels, per_device(): pl.pallas_call(functools.partial(kernel, counts, dims), out_shape=jax.Sha...  31.7 us
    unnamed x3, local copies, waits for them, and re-layouts  1.67 us

profile of v3, /device:TPU:0, one launch (start us, length us, event | category | flops | bytes accessed | tf_op | source)
XLA Modules:
  0.0 33.4 jit_solution(421848845092095650)
XLA Ops:
  0.0 0.0 copy-start
  0.0 0.7 %copy-done = f32[5,3,17]{2,1,0:T(4,128)S(1)} copy-done((f32[5,3,17]{2,1,0:T(4,128)S(1)}, f32[5,3,17]{2,1,0:T(4,128)}, u32[]{:S(2)}) %copy-start) | copy-done | bytes 1044
  0.7 31.7 %shard_map.28 = f32[32,64,128]{2,1,0:T(8,128)S(1)} custom-call(f32[5,3,17]{2,1,0:T(4,128)S(1)} %copy-done, f32[32,64,128]{2,1,0:T(8,128)} %x_hbm.1), custom_call_target="tpu_custom_call" | custom-call | tf_op jit(solution)/shard_map/pallas_call | solution.py:608
  32.4 1.0 %copy.4 = f32[32,64,128]{2,1,0:T(8,128)} copy(f32[32,64,128]{2,1,0:T(8,128)S(1)} %shard_map.28) | data formatting | bytes 2097152
Async XLA Ops:
  0.0 0.7 %copy-start = (f32[5,3,17]{2,1,0:T(4,128)S(1)}, f32[5,3,17]{2,1,0:T(4,128)}, u32[]{:S(2)}) copy-start(f32[5,3,17]{2,1,0:T(4,128)} %taps_hbm.1) | copy-start | bytes 3064

commit v4 on v2

--- a/solution.py
+++ b/solution.py
@@ -67,12 +67,18 @@
     return (v >= 0) & (v < n)
 
 
-def kernel(counts, dims, taps, x_ref, out_ref, e0, l0, r0, y0, y1, t1, t1l, t1r, e1, sw, f1, h1, h1l, h1r, d1, pr,
-           ua, am, v2, v2l, v2r, pq, yu, yd, xg, g2, u2, y2,
-           w0h, w0l, m0, w1h, w1l, m1, w2h, w2l, m2, c2, pz2, py2, py1, my2, wz2, ss, rs, sg, rg):
+def kernel(counts, dims, taps_hbm, x_hbm, out_ref, taps, x_ref, l0, r0, hy, hl, hr, zh, zl, relay, y0, y1, t1, t1l, t1r, e1, sw, f1, h1, h1l, h1r, d1, pr,
+           ua, am, v2, v2l, v2r, pq, yu, yd, xg, g2, z2h, z2l, y2,
+           w0h, w0l, m0, w1h, w1l, m1, w2h, w2l, m2, c2, pz2, py2, py1, my2, wz2, own_sem, ss, rs, sg, rg):
     nx, ny, nz = counts
     bx, by, bz = dims
     here = tuple(lax.axis_index(a) for a in AXES)
+    loads = [
+        pltpu.make_async_copy(x_hbm, x_ref, own_sem.at[0]),
+        pltpu.make_async_copy(taps_hbm, taps, own_sem.at[1]),
+    ]
+    for load in loads:
+        load.start()
     gx, gy, gz = here
     cx, cy, cz = bx // 2, by // 2, bz // 2
     fx, fy, fz = bx // 4, by // 4, bz // 4
@@ -108,8 +114,8 @@
             view[...] = jnp.zeros(view.shape, F32)
 
     every = slice(None)
-    clear(e0, (0, -1, 0), every, pl.ds(0, 8))
-    clear(e0, (0, 1, 0), every, pl.ds(8 + by, 8))
+    clear(hy, (0, -1, 0), every, pl.ds(0, 8))
+    clear(hy, (0, 1, 0), every, pl.ds(8, 8))
     clear(y0, (-1, 0, 0), pl.ds(0, 8))
     clear(y0, (1, 0, 0), pl.ds(8 + bx, 8))
     clear(t1l, (-1, 0, 0), every)
@@ -123,65 +129,9 @@
         ref[pl.ds(8 + bx, 8)] = jnp.zeros((8,) + ref.shape[1:], F32)
     am[pl.ds(0, 6)] = jnp.zeros((6,) + am.shape[1:], F32)
     am[pl.ds(cx + 9, 6)] = jnp.zeros((6,) + am.shape[1:], F32)
-    pl.semaphore_wait(barrier, total)
-
-    count = [0]
-
-    def remote(src, dst, d):
-        k = count[0]
-        count[0] += 1
-        copy = pltpu.make_async_remote_copy(
-            src_ref=src, dst_ref=dst, send_sem=ss.at[k], recv_sem=rs.at[k],
-            device_id=(gx + d[0], gy + d[1], gz + d[2]), device_id_type=pl.DeviceIdType.MESH,
-        )
-        return there(*d), there(-d[0], -d[1], -d[2]), copy
-
-    def start(copies):
-        for to, _, copy in copies:
-            pl.when(to)(copy.start)
-
-    def arrive(copies):
-        for _, fro, copy in copies:
-            pl.when(fro)(copy.wait_recv)
-
-    def left_over(copies):
-        for to, _, copy in copies:
-            pl.when(to)(copy.wait_send)
-
     right, left, ahead, behind, above, below = (
         (1, 0, 0), (-1, 0, 0), (0, 1, 0), (0, -1, 0), (0, 0, 1), (0, 0, -1)
     )
-    own_y = pl.ds(8, by)
-    ya = [
-        remote(x_ref.at[:, pl.ds(by - 8, 8)], e0.at[:, pl.ds(0, 8)], ahead),
-        remote(x_ref.at[:, pl.ds(0, 8)], e0.at[:, pl.ds(8 + by, 8)], behind),
-    ]
-    za = [remote(x_ref, l0.at[:, own_y], above), remote(x_ref, r0.at[:, own_y], below)]
-    zf = [
-        remote(e0.at[:, pl.ds(k, 8)], ref.at[:, pl.ds(k, 8)], d)
-        for k in (0, 8 + by) for ref, d in ((l0, above), (r0, below))
-    ]
-    z2 = [remote(v2, v2l, above), remote(v2, v2r, below)]
-    yp = [
-        remote(pq.at[:, pl.ds(fy, 8)], yu, ahead),
-        remote(pq.at[:, pl.ds(fy + 8, 8)], yd, behind),
-    ]
-    xa = [
-        [
-            remote(y0.at[pl.ds(bx + k, 2)], y0.at[pl.ds(k, 2)], right),
-            remote(y0.at[pl.ds(8 + k, 2)], y0.at[pl.ds(8 + bx + k, 2)], left),
-        ]
-        for k in range(0, 8, 2)
-    ]
-    xb = [remote(t1.at[pl.ds(half1 - 4, 6)], t1l, right), remote(t1.at[pl.ds(0, 6)], t1r, left)]
-    yb = [
-        remote(f1.at[:, pl.ds(cy, 16)], f1.at[:, pl.ds(0, 16)], ahead),
-        remote(f1.at[:, pl.ds(16, 16)], f1.at[:, pl.ds(16 + cy, 16)], behind),
-    ]
-    zb = [remote(h1, h1l, above), remote(h1, h1r, below)]
-    start(ya)
-    start(za)
-
     def put(h, l, v):
         hi, lo = split(v)
         h[...] = hi
@@ -214,27 +164,123 @@
     pos = jnp.where(i < bz + bz // 2, i, i - 2 * bz)
     put(wz2, None, jnp.where(j < fz, twice(pos, j, gz * cz, nz * cz), 0.0))
 
-    @pl.loop(0, bx // 2, unroll=4)
-    def _(c):
-        o = dot_left(my2, jnp.concatenate([x_ref[2 * c], x_ref[2 * c + 1]], axis=1), 2)
-        ua[8 + 2 * c] = o[:, :LANES]
-        ua[9 + 2 * c] = o[:, LANES:]
-
-    for m in range(-1, cx + 2):
-        am[m + 7] = restrict_x(ua, 8 + 2 * m) * inside(gx * cx + m, nx * cx).astype(F32)
-    for e in range(fx + 5):
-        v2[e] = restrict_x(am, 3 + 2 * e)
-    start(z2)
-
-    e0[:, own_y, :] = x_ref[...]
+    loads[1].wait()
     i, j = grids(2 * bz, bz)
     pos = jnp.where(i < bz + bz // 2, i, i - 2 * bz)
     k0 = pick(taps, 0, 2, pos - j + 8, inside(pos, bz + 8) | inside(pos + 8, 8))
     rz = cubic(pos - 2 * j, j < cz)
     put(w0h, w0l, jnp.concatenate([k0, rz], axis=1))
     i, j = grids(by + cy, by + 16)
+    j = jnp.where(j < by, j + 8, jnp.where(j < by + 8, j - by, j))
     stack(m0, jnp.where(i < by, pick(taps, 0, 1, j - i, i < by), cubic(j - 8 - 2 * (i - by), i >= by)), 3)
 
+    i, j = grids(2 * cz, LANES)
+    pos = jnp.where(i < cz + cz // 2, i, i - 2 * cz)
+    kk = j - 2
+    top = cz + 4
+    ok = (j < top) & inside(gz * cz + kk, nz * cz)
+    k1 = pick(taps, 1, 2, pos - kk + 8, ok)
+    i, j = grids(LANES, bz)
+    fine_z = cubic(j - 2 * (i - 2), i < top)
+    put(w1h, w1l, exact(k1, fine_z))
+    ry1 = up(cy + 4, 8)
+    i, j = grids(ry1, cy + 32)
+    ok = (i < cy + 4) & inside(gy * cy + i - 2, ny * cy)
+    stack(m1, pick(taps, 1, 1, j - 16 - (i - 2) + 8, ok), 3)
+    i, j = grids(by, up(ry1, 16))
+    stack(py1, cubic(i - 2 * (j - 2), j < cy + 4), 2)
+
+    loads[0].wait()
+
+    @pl.loop(0, bx // 2, unroll=4)
+    def _(c):
+        o = dot_left(my2, jnp.concatenate([x_ref[2 * c], x_ref[2 * c + 1]], axis=1), 2)
+        ua[8 + 2 * c] = o[:, :LANES]
+        ua[9 + 2 * c] = o[:, LANES:]
+
+    for m in range(-1, cx + 2):
+        am[m + 7] = restrict_x(ua, 8 + 2 * m) * inside(gx * cx + m, nx * cx).astype(F32)
+    for e in range(fx + 5):
+        v2[e] = restrict_x(am, 3 + 2 * e)
+    pl.semaphore_wait(barrier, total)
+
+    count = [0]
+
+    def remote(src, dst, d, to=None, fro=None):
+        k = count[0]
+        count[0] += 1
+        copy = pltpu.make_async_remote_copy(
+            src_ref=src, dst_ref=dst, send_sem=ss.at[k], recv_sem=rs.at[k],
+            device_id=(gx + d[0], gy + d[1], gz + d[2]), device_id_type=pl.DeviceIdType.MESH,
+        )
+        to = there(*d) if to is None else to
+        fro = there(-d[0], -d[1], -d[2]) if fro is None else fro
+        return to, fro, copy
+
+    def start(copies):
+        for to, _, copy in copies:
+            pl.when(to)(copy.start)
+
+    def arrive(copies):
+        for _, fro, copy in copies:
+            pl.when(fro)(copy.wait_recv)
+
+    def left_over(copies):
+        for to, _, copy in copies:
+            pl.when(to)(copy.wait_send)
+
+    ends = (pl.ds(0, 8), pl.ds(bx - 8, 8)), (pl.ds(8, bx - 16),)
+    ya, zf = [], []
+    for xs in ends:
+        ya.append([
+            remote(x_ref.at[x, pl.ds(by - 8, 8)], hy.at[x, pl.ds(0, 8)], ahead) for x in xs
+        ] + [
+            remote(x_ref.at[x, pl.ds(0, 8)], hy.at[x, pl.ds(8, 8)], behind) for x in xs
+        ])
+        zf.append([remote(hy.at[x], hl.at[x], above) for x in xs] + [remote(hy.at[x], hr.at[x], below) for x in xs])
+    za = [remote(x_ref, l0, above), remote(x_ref, r0, below)]
+    z2 = [remote(v2, v2l, above), remote(v2, v2r, below)]
+    yp = [
+        remote(pq.at[:, pl.ds(fy, 8)], yu, ahead),
+        remote(pq.at[:, pl.ds(fy + 8, 8)], yd, behind),
+    ]
+    mid_l, mid_r = (gx == 1, gx == 2) if nx == 4 else (jnp.bool_(False), jnp.bool_(False))
+    end_l, end_r = (gx == 0, gx == 3) if nx == 4 else (jnp.bool_(False), jnp.bool_(False))
+    near, rest = 2, 6
+
+    def to_left(k, n, **ok):
+        return remote(y0.at[pl.ds(8 + k, n)], y0.at[pl.ds(8 + bx + k, n)], left, **ok)
+
+    def to_right(k, n, **ok):
+        return remote(y0.at[pl.ds(bx + k, n)], y0.at[pl.ds(k, n)], right, **ok)
+
+    xa = [
+        [to_left(0, near)],
+        [
+            to_left(near, rest, to=there(*left) & jnp.logical_not(mid_r), fro=there(*right) & jnp.logical_not(mid_l)),
+            to_right(0, near),
+            to_right(near, rest, to=there(*right) & jnp.logical_not(mid_l), fro=there(*left) & jnp.logical_not(mid_r)),
+        ],
+    ]
+    hop1, hop2 = [], []
+    if nx == 4:
+        hop1 = [
+            remote(y0.at[pl.ds(bx + near, rest)], relay, (2, 0, 0), to=mid_l, fro=end_r),
+            remote(y0.at[pl.ds(8 + near, rest)], relay, (-2, 0, 0), to=mid_r, fro=end_l),
+        ]
+        hop2 = [
+            remote(relay, y0.at[pl.ds(near, rest)], left, to=end_r, fro=mid_r),
+            remote(relay, y0.at[pl.ds(8 + bx + near, rest)], right, to=end_l, fro=mid_l),
+        ]
+    xb = [remote(t1.at[pl.ds(0, 6)], t1r, left), remote(t1.at[pl.ds(half1 - 4, 6)], t1l, right)]
+    yb = [
+        remote(f1.at[:, pl.ds(cy, 16)], f1.at[:, pl.ds(0, 16)], ahead),
+        remote(f1.at[:, pl.ds(16, 16)], f1.at[:, pl.ds(16 + cy, 16)], behind),
+    ]
+    zb = [remote(h1, h1l, above), remote(h1, h1r, below)]
+    start(z2)
+    start(ya[0])
+    start(za)
     arrive(z2)
     parts = []
     for e in range(fx + 5):
@@ -252,22 +298,7 @@
         pq[g] = acc
     start(yp)
 
-    i, j = grids(2 * cz, LANES)
-    pos = jnp.where(i < cz + cz // 2, i, i - 2 * cz)
-    kk = j - 2
-    top = cz + 4
-    ok = (j < top) & inside(gz * cz + kk, nz * cz)
-    k1 = pick(taps, 1, 2, pos - kk + 8, ok)
-    i, j = grids(LANES, bz)
-    fine_z = cubic(j - 2 * (i - 2), i < top)
-    put(w1h, w1l, exact(k1, fine_z))
-    ry1 = up(cy + 4, 8)
-    i, j = grids(ry1, cy + 32)
-    ok = (i < cy + 4) & inside(gy * cy + i - 2, ny * cy)
-    stack(m1, pick(taps, 1, 1, j - 16 - (i - 2) + 8, ok), 3)
-    i, j = grids(by, up(ry1, 16))
-    stack(py1, cubic(i - 2 * (j - 2), j < cy + 4), 2)
-
+    start(ya[1])
     def plain(axis, level, n, pad, turned):
         i, j = grids(pad, pad)
         d = (i - j if turned else j - i) + 8
@@ -297,7 +328,12 @@
     tz = 40
     ops = operators(2, n2z, gz * fz - 2, tz, ez)
     cols = jnp.concatenate(list(ops) + [jnp.zeros((LANES - 3 * tz, ops[0].shape[1]), F32)], axis=0)
-    put(w2h, w2l, cols.T)
+    hi, lo = split(cols.T)
+    for ref, v in ((w2h, hi), (w2l, lo)):
+        ref[...] = jnp.zeros(ref.shape, BF16)
+        for b in range(nz):
+            for k in range(per):
+                ref[pl.ds(b * LANES + k * fz, fz), pl.ds(k * LANES, LANES)] = v[b * fz:(b + 1) * fz]
     ty = up(ey, 8)
     ops = operators(1, n2y, gy * fy - 2, ty, ey)
     stack(m2, jnp.concatenate(list(ops), axis=0)[:, :n2y], 3)
@@ -313,15 +349,8 @@
     put(pz2, None, exact(e1_z, fine_z))
     i, j = grids(ry1, up(ty, 16))
     stack(py2, cubic((i - 2) - 2 * (j - 2), (j < ey) & (i < cy + 4) & inside(gy * cy + i - 2, ny * cy)), 2)
-    arrive(ya)
-    start(zf)
-    arrive(za)
-    arrive(yp)
-    own = [pq[:, pl.ds(0, 8)] + yu[...]]
-    if fy > 16:
-        own.append(pq[:, pl.ds(8, fy - 16)])
-    own.append(pq[:, pl.ds(fy - 8, 8)] + yd[...])
-    xg[gx] = jnp.concatenate(own, axis=1)
+    arrive(ya[0])
+    start(zf[0])
     def spread(dim, n, ref, k0):
         out = []
         for m, d in enumerate([d for d in range(-(n - 1), n) if d]):
@@ -349,32 +378,81 @@
         for _, fro, _, land in copies:
             pl.when(fro)(land.wait_recv)
 
+    arrive(yp)
+    own = [pq[:, pl.ds(0, 8)] + yu[...]]
+    if fy > 16:
+        own.append(pq[:, pl.ds(8, fy - 16)])
+    own.append(pq[:, pl.ds(fy - 8, 8)] + yd[...])
+    xg[gx] = jnp.concatenate(own, axis=1)
     ca = spread(0, nx, lambda k: xg.at[k], 0)
     begin(ca)
-    arrive(zf)
-
-    wide = by + 16
+
+
     step0 = 4
 
-    def level0(c):
+    def across(own, lo, hi):
+        rows = own.shape[0] * own.shape[1]
+        other = jnp.where(
+            mask_r, hi.reshape(rows, LANES), jnp.where(mask_l, lo.reshape(rows, LANES), 0.0)
+        )
+        v = jnp.concatenate([own.reshape(rows, LANES), other], axis=1)
+        return split(dot_right(v, (w0h, w0l)))
+
+    def level0_own(c):
         at = pl.ds(c * step0, step0)
-        own = e0[at].reshape(step0 * wide, LANES)
-        other = jnp.where(
-            mask_r, r0[at].reshape(step0 * wide, LANES),
-            jnp.where(mask_l, l0[at].reshape(step0 * wide, LANES), 0.0),
-        )
-        v = dot_right(jnp.concatenate([own, other], axis=1), (w0h, w0l))
-        for k in range(step0):
-            o = dot_left(m0, v[k * wide:(k + 1) * wide], 3)
-            y0[8 + c * step0 + k] = o[:by, :LANES]
-            y1[8 + c * step0 + k] = o[by:, LANES:]
-
+        hi, lo = across(x_ref[at], l0[at], r0[at])
+        zh[at, pl.ds(0, by), :] = hi.reshape(step0, by, 2 * LANES)
+        zl[at, pl.ds(0, by), :] = lo.reshape(step0, by, 2 * LANES)
+
+    def level0_halo(x, n):
+        at = pl.ds(x, n)
+        hi, lo = across(hy[at], hl[at], hr[at])
+        zh[at, pl.ds(by, 16), :] = hi.reshape(n, 16, 2 * LANES)
+        zl[at, pl.ds(by, 16), :] = lo.reshape(n, 16, 2 * LANES)
+
+    def level0(k):
+        hi = zh[k]
+        o = mm(m0[...], jnp.concatenate([hi, zl[k], hi], axis=0))
+        y0[8 + k] = o[:by, :LANES]
+        y1[8 + k] = o[by:, LANES:]
+
+    arrive(za)
     edge = 8 // step0
     for c in range(edge):
-        level0(c)
-        level0(bx // step0 - edge + c)
+        level0_own(c)
+        level0_own(bx // step0 - edge + c)
+    pl.loop(edge, bx // step0 - edge, unroll=4)(level0_own)
+    arrive(ya[1])
+    start(zf[1])
+    arrive(zf[0])
+    level0_halo(0, 8)
+    level0_halo(bx - 8, 8)
+    for k in range(8):
+        level0(k)
+        level0(bx - 8 + k)
     start(xa[0])
-    pl.loop(edge, bx // step0 - edge, unroll=True)(level0)
+    start(hop1)
+    arrive(zf[1])
+    level0_halo(8, bx - 16)
+    pl.loop(8, bx - 8, unroll=8)(level0)
+
+    for p in range(half1 + 2):
+        a = restrict_x(y1, 4 + 4 * p)
+        b = restrict_x(y1, 6 + 4 * p)
+        t1[p] = jnp.where(lane < cz, a, pltpu.roll(b, cz, 1))
+    start(xb)
+    start(xa[1])
+
+    def conv0(p, ts):
+        acc = None
+        for t in ts:
+            v = taps[0, 0, t] * y0[p + t]
+            acc = v if acc is None else acc + v
+        return acc
+
+    @pl.loop(8, bx - 8)
+    def _(p):
+        out_ref[p] = conv0(p, range(17))
 
     landed(ca)
     for m in range(np2 * nx):
@@ -387,22 +465,11 @@
     cb = spread(1, ny, lambda k: g2.at[gz, k], 0)
     begin(cb)
 
-    for p in range(half1 + 2):
-        a = restrict_x(y1, 4 + 4 * p)
-        b = restrict_x(y1, 6 + 4 * p)
-        t1[p] = jnp.where(lane < cz, a, pltpu.roll(b, cz, 1))
-    start(xb)
-    for k in range(1, 4):
-        start(xa[k])
-
-    def conv0(p):
-        acc = taps[0, 0, 0] * y0[p]
-        for t in range(1, 17):
-            acc = acc + taps[0, 0, t] * y0[p + t]
-        out_ref[p] = acc
-
-    pl.loop(8, bx - 8)(conv0)
-
+    for p in range(8):
+        out_ref[p] = conv0(p, range(8 - p, 17))
+        out_ref[bx - 8 + p] = conv0(bx - 8 + p, range(16 - p))
+    arrive(hop1)
+    start(hop2)
     arrive(xb)
     n1 = half1 + 10
     to_l, to_r = there(*left).astype(F32), there(*right).astype(F32)
@@ -434,45 +501,34 @@
     landed(cb)
     cc = spread(2, nz, lambda k: g2.at[k], 0)
     begin(cc)
+    landed(cc)
+    seen = lambda r: inside(gx * cx + r - 2, nx * cx).astype(F32)
+    batch = max(1, min(nx * np2, 256 // n2y))
+    for m in range(0, nx * np2, batch):
+        v = jnp.concatenate([
+            jnp.concatenate([g2[b, :, k].reshape(n2y, LANES) for b in range(nz)], axis=1)
+            for k in range(m, m + batch)
+        ], axis=0)
+        hi, lo = split(dot_right(v, (w2h, w2l)))
+        z2h[pl.ds(m, batch)] = hi.reshape(batch, n2y, per * LANES)
+        z2l[pl.ds(m, batch)] = lo.reshape(batch, n2y, per * LANES)
+
+    @pl.loop(0, nx * np2, unroll=4)
+    def _(m):
+        hi = z2h[m]
+        o = mm(m2[...], jnp.concatenate([hi, z2l[m], hi], axis=0))
+        for k in range(per):
+            w = o[:, k * LANES:(k + 1) * LANES]
+            y2[per * m + k] = jnp.where(
+                lane < tz, w[:ty], jnp.where(lane < 2 * tz, w[ty:2 * ty], w[2 * ty:])
+            )
+
     arrive(yb)
     for q in range(0, half1 + 2, 2):
         o = dot_left(m1, jnp.concatenate([f1[q], f1[q + 1]], axis=1), 3)
         h1[q] = o[:, :LANES]
         h1[q + 1] = o[:, LANES:]
     start(zb)
-    landed(cc)
-    seen = lambda r: inside(gx * cx + r - 2, nx * cx).astype(F32)
-    tiles = u2.shape[0]
-
-    @pl.loop(0, nx * np2)
-    def _(p):
-        for b in range(ny):
-            for k in range(per):
-                for t in range(tiles):
-                    acc = jnp.zeros((fy, LANES), F32)
-                    for s in range(t * per, min(nz, (t + 1) * per)):
-                        v = g2[s, b, p]
-                        sh = (fz * (s - t * per - k)) % LANES
-                        v = pltpu.roll(v, sh, 1) if sh else v
-                        lo = fz * (s - t * per)
-                        acc = jnp.where((lane >= lo) & (lane < lo + fz), v, acc)
-                    u2[t, p * per + k, pl.ds(b * fy, fy), :] = acc
-
-    step2 = 2
-
-    @pl.loop(0, n2x // step2, unroll=U2)
-    def _(c):
-        at = pl.ds(c * step2, step2)
-        v = jnp.concatenate([u2[t, at].reshape(step2 * n2y, LANES) for t in range(tiles)], axis=1)
-        v = dot_right(v, (w2h, w2l))
-        v = jnp.concatenate([v[k * n2y:(k + 1) * n2y] for k in range(step2)], axis=1)
-        o = dot_left(m2, v, 3)
-        for k in range(step2):
-            w = o[:, k * LANES:(k + 1) * LANES]
-            y2[c * step2 + k] = jnp.where(
-                lane < tz, w[:ty], jnp.where(lane < 2 * tz, w[ty:2 * ty], w[2 * ty:])
-            )
-
     parts = []
     for r in range(ex):
         acc = c2[r, pl.ds(0, 1)] * y2[0]
@@ -488,13 +544,13 @@
             w = jnp.concatenate([w, jnp.zeros((fill, LANES), F32)], axis=0)
         pro.append(dot_left(py2, w, 2))
     arrive(zb)
-    near = lax.rem(lane, cz) < cz // 2
+    inner = lax.rem(lane, cz) < cz // 2
     step1 = 5 if (half1 + 2) % 5 == 0 else 1
     for c in range(0, half1 + 2, step1):
         parts = []
         for q in range(c, c + step1):
             own = h1[q]
-            other = jnp.where(near & has_r, h1r[q], jnp.where(jnp.logical_not(near) & has_l, h1l[q], 0.0))
+            other = jnp.where(inner & has_r, h1r[q], jnp.where(jnp.logical_not(inner) & has_l, h1l[q], 0.0))
             parts.append(jnp.where(lane < cz, own, pltpu.roll(other, cz, 1)))
             parts.append(jnp.where(lane < cz, pltpu.roll(own, cz, 1), other))
         v = dot_right(jnp.concatenate(parts, axis=0), (w1h, w1l))
@@ -519,10 +575,11 @@
         pr[2 * c] = o[:, :LANES]
         pr[2 * c + 1] = o[:, LANES:]
 
-    for group in xa:
+    for group in (*xa, hop2):
         arrive(group)
-    pl.loop(0, 8)(conv0)
-    pl.loop(bx - 8, bx)(conv0)
+    for p in range(8):
+        out_ref[p] = out_ref[p] + conv0(p, range(8 - p))
+        out_ref[bx - 8 + p] = out_ref[bx - 8 + p] + conv0(bx - 8 + p, range(16 - p, 17))
 
     @pl.loop(0, cx)
     def _(m):
@@ -532,7 +589,7 @@
             0.5625 * (pr[at] + pr[at + 1]) - 0.0625 * (pr[at - 1] + pr[at + 2])
         )
 
-    for group in (ya, za, zf, z2, yp, *xa, xb, yb, zb):
+    for group in (*ya, za, *zf, z2, yp, *xa, hop1, hop2, xb, yb, zb):
         left_over(group)
     for group in (ca, cb, cc):
         for to, _, copy, _ in group:
@@ -546,19 +603,20 @@
     cx, cy, cz = bx // 2, by // 2, bz // 2
     fx, fy, fz = bx // 4, by // 4, bz // 4
     n2x, n2y, n2z = nx * fx, ny * fy, nz * fz
-    np2 = fx // (LANES // fz)
+    per = LANES // fz
+    np2 = fx // per
     half1 = cx // 2
     ry1 = up(cy + 4, 8)
     ty = up(fy + 5, 8)
-    tiles = up(n2z, LANES) // LANES
     V = pltpu.VMEM
-    ext0 = (bx, by + 16, LANES)
     wide = max(nx, ny, nz) * 2
     dma = pltpu.SemaphoreType.DMA
     row = lambda n, r: V((n, r, LANES), F32)
     scratch = [
-        V(ext0, F32), V(ext0, F32), V(ext0, F32),
-        row(bx + 16, by), row(bx + 16, cy),
+        pltpu.SMEM(kernel_taps.shape, F32), V(dims, F32),
+        row(bx, by), row(bx, by), row(bx, 16), row(bx, 16), row(bx, 16),
+        V((bx, by + 16, 2 * LANES), BF16), V((bx, by + 16, 2 * LANES), BF16),
+        row(6, by), row(bx + 16, by), row(bx + 16, cy),
         row(half1 + 2, cy), row(6, cy), row(6, cy), row(half1 + 10, cy), row(half1 + 9, cy),
         row(half1 + 2, cy + 32), row(half1 + 2, ry1), row(half1 + 2, ry1), row(half1 + 2, ry1),
         row(cx + 4, ry1), row(cx + 4, by),
@@ -567,28 +625,28 @@
         row(np2 + 2, fy + 16), row(np2 + 2, 8), row(np2 + 2, 8),
         V((nx, np2 + 2, fy, LANES), F32),
         V((nz, ny, nx * np2, fy, LANES), F32),
-        V((tiles, n2x, n2y, LANES), F32),
+        V((nx * np2, n2y, per * LANES), BF16), V((nx * np2, n2y, per * LANES), BF16),
         row(n2x, ty),
         V((2 * bz, bz + LANES), BF16), V((2 * bz, bz + LANES), BF16),
         V((by + cy, 3 * (by + 16)), BF16),
         V((2 * cz, bz), BF16), V((2 * cz, bz), BF16),
         V((ry1, 3 * (cy + 32)), BF16),
-        V((tiles * LANES, LANES), BF16), V((tiles * LANES, LANES), BF16),
+        V((nz * LANES, per * LANES), BF16), V((nz * LANES, per * LANES), BF16),
         V((3 * ty, 3 * n2y), BF16),
         row(fx + 5, n2x),
         V((LANES, bz), BF16), V((ry1, 2 * up(ty, 16)), BF16),
         V((by, 2 * up(ry1, 16)), BF16),
         V((fy + 16, 2 * by), BF16), V((2 * bz, LANES), BF16),
-        dma((32,)), dma((32,)), dma((3, wide)), dma((3, wide)),
+        dma((2,)), dma((32,)), dma((32,)), dma((3, wide)), dma((3, wide)),
     ]
     return pl.pallas_call(
         functools.partial(kernel, counts, dims),
         out_shape=jax.ShapeDtypeStruct(dims, F32),
-        in_specs=[pl.BlockSpec(memory_space=pltpu.SMEM), pl.BlockSpec(memory_space=pltpu.VMEM)],
+        in_specs=[pl.BlockSpec(memory_space=pltpu.HBM)] * 2,
         out_specs=pl.BlockSpec(memory_space=pltpu.VMEM),
         scratch_shapes=scratch,
         compiler_params=pltpu.CompilerParams(
-            collective_id=0, has_side_effects=True, vmem_limit_bytes=28 * 2**20
+            collective_id=0, has_side_effects=True, vmem_limit_bytes=105 * 2**19
         ),
     )(kernel_taps, charges)
 

time: 39.5 us -> 28.5 us (0.72)
  Pallas kernels: 36.4 us -> 26.6 us
  local copies, waits for them, and re-layouts: 2.9 us -> 1.67 us
    pallas_call x1, Pallas kernels: 36.4 us -> 26.6 us  [per_device(): pl.pallas_call(functools.partial(kernel, counts, dims), out_shape=jax.Sha...]
    unnamed x5 -> x3, local copies, waits for them, and re-layouts: 2.9 us -> 1.67 us
where the time goes in v4:
time: 28.5 us; the launch traced here: 28.3 us
  Pallas kernels  26.6 us (93%)
  local copies, waits for them, and re-layouts  1.67 us (6%)
    pallas_call x1, Pallas kernels, per_device(): pl.pallas_call(functools.partial(kernel, counts, dims), out_shape=jax.Sha...  26.6 us
    unnamed x3, local copies, waits for them, and re-layouts  1.67 us

profile of v4, /device:TPU:0, one launch (start us, length us, event | category | flops | bytes accessed | tf_op | source)
XLA Modules:
  0.0 28.3 jit_solution(15866233798613374128)
XLA Ops:
  0.0 0.0 copy-start
  0.0 0.7 %copy-done = f32[5,3,17]{2,1,0:T(4,128)S(1)} copy-done((f32[5,3,17]{2,1,0:T(4,128)S(1)}, f32[5,3,17]{2,1,0:T(4,128)}, u32[]{:S(2)}) %copy-start) | copy-done | bytes 1044
  0.7 26.6 %shard_map.28 = f32[32,64,128]{2,1,0:T(8,128)S(1)} custom-call(f32[5,3,17]{2,1,0:T(4,128)S(1)} %copy-done, f32[32,64,128]{2,1,0:T(8,128)} %x_hbm.1), custom_call_target="tpu_custom_call" | custom-call | tf_op jit(solution)/shard_map/pallas_call | solution.py:642
  27.3 1.0 %copy.4 = f32[32,64,128]{2,1,0:T(8,128)} copy(f32[32,64,128]{2,1,0:T(8,128)S(1)} %shard_map.28) | data formatting | bytes 2097152
Async XLA Ops:
  0.0 0.7 %copy-start = (f32[5,3,17]{2,1,0:T(4,128)S(1)}, f32[5,3,17]{2,1,0:T(4,128)}, u32[]{:S(2)}) copy-start(f32[5,3,17]{2,1,0:T(4,128)} %taps_hbm.1) | copy-start | bytes 3064

commit v5 on v3

--- a/solution.py
+++ b/solution.py
@@ -67,16 +67,17 @@
     return (v >= 0) & (v < n)
 
 
-def kernel(counts, dims, taps_hbm, x_hbm, out_ref, taps, x_ref, l0, r0, hy, hl, hr, zh, zl, y0, y1, t1, t1l, t1r, e1, sw, f1, h1, h1l, h1r, d1, pr,
+def kernel(counts, dims, taps_hbm, x_hbm, out_ref, taps, x_ref, l0, r0, hy, hl, hr, zh, zl, relay, y0, y1, t1, t1l, t1r, e1, sw, f1, h1, h1l, h1r, d1, pr,
            ua, am, v2, v2l, v2r, pq, yu, yd, xg, g2, z2h, z2l, y2,
            w0h, w0l, m0, w1h, w1l, m1, w2h, w2l, m2, c2, pz2, py2, py1, my2, wz2, own_sem, ss, rs, sg, rg):
     nx, ny, nz = counts
     bx, by, bz = dims
     here = tuple(lax.axis_index(a) for a in AXES)
     loads = [
-        pltpu.make_async_copy(x_hbm, x_ref, own_sem.at[0]),
-        pltpu.make_async_copy(taps_hbm, taps, own_sem.at[1]),
+        pltpu.make_async_copy(x_hbm.at[pl.ds(k, bx // 4)], x_ref.at[pl.ds(k, bx // 4)], own_sem.at[4 * k // bx])
+        for k in range(0, bx, bx // 4)
     ]
+    loads.append(pltpu.make_async_copy(taps_hbm, taps, own_sem.at[4]))
     for load in loads:
         load.start()
     gx, gy, gz = here
@@ -129,20 +130,67 @@
         ref[pl.ds(8 + bx, 8)] = jnp.zeros((8,) + ref.shape[1:], F32)
     am[pl.ds(0, 6)] = jnp.zeros((6,) + am.shape[1:], F32)
     am[pl.ds(cx + 9, 6)] = jnp.zeros((6,) + am.shape[1:], F32)
-    for load in loads:
-        load.wait()
+    right, left, ahead, behind, above, below = (
+        (1, 0, 0), (-1, 0, 0), (0, 1, 0), (0, -1, 0), (0, 0, 1), (0, 0, -1)
+    )
+    def put(h, l, v):
+        hi, lo = split(v)
+        h[...] = hi
+        if l is not None:
+            l[...] = lo
+
+    def stack(ref, v, terms):
+        hi, lo = split(v)
+        ref[...] = jnp.concatenate([hi, hi, lo][:terms], axis=1)
+
+    def twice(pos, at, base, n):
+        out = jnp.zeros(pos.shape, F32)
+        for k, w in ((-3, -0.0625), (-1, 0.5625), (0, 1.0), (1, 0.5625), (3, -0.0625)):
+            m = 2 * at + k
+            out = out + w * cubic(pos - 2 * m, inside(base + m, n))
+        return out
+
+    def restrict_x(ref, at):
+        return (
+            ref[at] + 0.5625 * (ref[at - 1] + ref[at + 1]) - 0.0625 * (ref[at - 3] + ref[at + 3])
+        )
+
+    lane = lax.broadcasted_iota(jnp.int32, (1, LANES), 1)
+    has_r, has_l = there(*above), there(*below)
+    mask_r, mask_l = (lane < LANES // 2) & has_r, (lane >= LANES // 2) & has_l
+    rows2 = fy + 16
+    i, j = grids(rows2, by)
+    stack(my2, twice(j, jnp.where(i < fy + 8, i, i - rows2), gy * cy, ny * cy), 2)
+    i, j = grids(2 * bz, LANES)
+    pos = jnp.where(i < bz + bz // 2, i, i - 2 * bz)
+    put(wz2, None, jnp.where(j < fz, twice(pos, j, gz * cz, nz * cz), 0.0))
+
+
+    for k in range(4):
+        loads[k].wait()
+        for c in range(k * (bx // 8), (k + 1) * (bx // 8)):
+            o = dot_left(my2, jnp.concatenate([x_ref[2 * c], x_ref[2 * c + 1]], axis=1), 2)
+            ua[8 + 2 * c] = o[:, :LANES]
+            ua[9 + 2 * c] = o[:, LANES:]
+
+    for m in range(-1, cx + 2):
+        am[m + 7] = restrict_x(ua, 8 + 2 * m) * inside(gx * cx + m, nx * cx).astype(F32)
+    for e in range(fx + 5):
+        v2[e] = restrict_x(am, 3 + 2 * e)
     pl.semaphore_wait(barrier, total)
 
     count = [0]
 
-    def remote(src, dst, d):
+    def remote(src, dst, d, to=None, fro=None):
         k = count[0]
         count[0] += 1
         copy = pltpu.make_async_remote_copy(
             src_ref=src, dst_ref=dst, send_sem=ss.at[k], recv_sem=rs.at[k],
             device_id=(gx + d[0], gy + d[1], gz + d[2]), device_id_type=pl.DeviceIdType.MESH,
         )
-        return there(*d), there(-d[0], -d[1], -d[2]), copy
+        to = there(*d) if to is None else to
+        fro = there(-d[0], -d[1], -d[2]) if fro is None else fro
+        return to, fro, copy
 
     def start(copies):
         for to, _, copy in copies:
@@ -156,9 +204,6 @@
         for to, _, copy in copies:
             pl.when(to)(copy.wait_send)
 
-    right, left, ahead, behind, above, below = (
-        (1, 0, 0), (-1, 0, 0), (0, 1, 0), (0, -1, 0), (0, 0, 1), (0, 0, -1)
-    )
     ends = (pl.ds(0, 8), pl.ds(bx - 8, 8)), (pl.ds(8, bx - 16),)
     ya, zf = [], []
     for xs in ends:
@@ -174,67 +219,45 @@
         remote(pq.at[:, pl.ds(fy, 8)], yu, ahead),
         remote(pq.at[:, pl.ds(fy + 8, 8)], yd, behind),
     ]
+    mid_l, mid_r = (gx == 1, gx == 2) if nx == 4 else (jnp.bool_(False), jnp.bool_(False))
+    end_l, end_r = (gx == 0, gx == 3) if nx == 4 else (jnp.bool_(False), jnp.bool_(False))
+    near, rest = 3, 5
+
+    def to_left(k, n, **ok):
+        return remote(y0.at[pl.ds(8 + k, n)], y0.at[pl.ds(8 + bx + k, n)], left, **ok)
+
+    def to_right(k, n, **ok):
+        return remote(y0.at[pl.ds(bx + k, n)], y0.at[pl.ds(k, n)], right, **ok)
+
     xa = [
+        [to_left(0, 1), to_right(0, 1)],
         [
-            remote(y0.at[pl.ds(bx + k, n)], y0.at[pl.ds(k, n)], right),
-            remote(y0.at[pl.ds(8 + k, n)], y0.at[pl.ds(8 + bx + k, n)], left),
+            to_left(1, near - 1),
+            to_left(near, rest, to=there(*left) & jnp.logical_not(mid_r), fro=there(*right) & jnp.logical_not(mid_l)),
+            to_right(1, near - 1),
+            to_right(near, rest, to=there(*right) & jnp.logical_not(mid_l), fro=there(*left) & jnp.logical_not(mid_r)),
+        ],
+    ]
+    hop1, hop2 = [], []
+    if nx == 4:
+        hop1 = [
+            remote(y0.at[pl.ds(bx + near, rest)], relay, (2, 0, 0), to=mid_l, fro=end_r),
+            remote(y0.at[pl.ds(8 + near, rest)], relay, (-2, 0, 0), to=mid_r, fro=end_l),
         ]
-        for k, n in ((0, 2), (2, 6))
-    ]
-    xb = [remote(t1.at[pl.ds(half1 - 4, 6)], t1l, right), remote(t1.at[pl.ds(0, 6)], t1r, left)]
+        hop2 = [
+            remote(relay, y0.at[pl.ds(near, rest)], left, to=end_r, fro=mid_r),
+            remote(relay, y0.at[pl.ds(8 + bx + near, rest)], right, to=end_l, fro=mid_l),
+        ]
+    xb = [remote(t1.at[pl.ds(0, 6)], t1r, left), remote(t1.at[pl.ds(half1 - 4, 6)], t1l, right)]
     yb = [
         remote(f1.at[:, pl.ds(cy, 16)], f1.at[:, pl.ds(0, 16)], ahead),
         remote(f1.at[:, pl.ds(16, 16)], f1.at[:, pl.ds(16 + cy, 16)], behind),
     ]
     zb = [remote(h1, h1l, above), remote(h1, h1r, below)]
+    start(z2)
     start(ya[0])
     start(za)
-    start(ya[1])
-
-    def put(h, l, v):
-        hi, lo = split(v)
-        h[...] = hi
-        if l is not None:
-            l[...] = lo
-
-    def stack(ref, v, terms):
-        hi, lo = split(v)
-        ref[...] = jnp.concatenate([hi, hi, lo][:terms], axis=1)
-
-    def twice(pos, at, base, n):
-        out = jnp.zeros(pos.shape, F32)
-        for k, w in ((-3, -0.0625), (-1, 0.5625), (0, 1.0), (1, 0.5625), (3, -0.0625)):
-            m = 2 * at + k
-            out = out + w * cubic(pos - 2 * m, inside(base + m, n))
-        return out
-
-    def restrict_x(ref, at):
-        return (
-            ref[at] + 0.5625 * (ref[at - 1] + ref[at + 1]) - 0.0625 * (ref[at - 3] + ref[at + 3])
-        )
-
-    lane = lax.broadcasted_iota(jnp.int32, (1, LANES), 1)
-    has_r, has_l = there(*above), there(*below)
-    mask_r, mask_l = (lane < LANES // 2) & has_r, (lane >= LANES // 2) & has_l
-    rows2 = fy + 16
-    i, j = grids(rows2, by)
-    stack(my2, twice(j, jnp.where(i < fy + 8, i, i - rows2), gy * cy, ny * cy), 2)
-    i, j = grids(2 * bz, LANES)
-    pos = jnp.where(i < bz + bz // 2, i, i - 2 * bz)
-    put(wz2, None, jnp.where(j < fz, twice(pos, j, gz * cz, nz * cz), 0.0))
-
-    @pl.loop(0, bx // 2, unroll=4)
-    def _(c):
-        o = dot_left(my2, jnp.concatenate([x_ref[2 * c], x_ref[2 * c + 1]], axis=1), 2)
-        ua[8 + 2 * c] = o[:, :LANES]
-        ua[9 + 2 * c] = o[:, LANES:]
-
-    for m in range(-1, cx + 2):
-        am[m + 7] = restrict_x(ua, 8 + 2 * m) * inside(gx * cx + m, nx * cx).astype(F32)
-    for e in range(fx + 5):
-        v2[e] = restrict_x(am, 3 + 2 * e)
-    start(z2)
-
+    loads[4].wait()
     i, j = grids(2 * bz, bz)
     pos = jnp.where(i < bz + bz // 2, i, i - 2 * bz)
     k0 = pick(taps, 0, 2, pos - j + 8, inside(pos, bz + 8) | inside(pos + 8, 8))
@@ -244,39 +267,22 @@
     j = jnp.where(j < by, j + 8, jnp.where(j < by + 8, j - by, j))
     stack(m0, jnp.where(i < by, pick(taps, 0, 1, j - i, i < by), cubic(j - 8 - 2 * (i - by), i >= by)), 3)
 
-    step0 = 4
-
-    def across(own, lo, hi):
-        rows = own.shape[0] * own.shape[1]
-        other = jnp.where(
-            mask_r, hi.reshape(rows, LANES), jnp.where(mask_l, lo.reshape(rows, LANES), 0.0)
-        )
-        v = jnp.concatenate([own.reshape(rows, LANES), other], axis=1)
-        return split(dot_right(v, (w0h, w0l)))
-
-    def level0_own(c):
-        at = pl.ds(c * step0, step0)
-        hi, lo = across(x_ref[at], l0[at], r0[at])
-        zh[at, pl.ds(0, by), :] = hi.reshape(step0, by, 2 * LANES)
-        zl[at, pl.ds(0, by), :] = lo.reshape(step0, by, 2 * LANES)
-
-    def level0_halo(x, n):
-        at = pl.ds(x, n)
-        hi, lo = across(hy[at], hl[at], hr[at])
-        zh[at, pl.ds(by, 16), :] = hi.reshape(n, 16, 2 * LANES)
-        zl[at, pl.ds(by, 16), :] = lo.reshape(n, 16, 2 * LANES)
-
-    def level0(k):
-        hi = zh[k]
-        o = mm(m0[...], jnp.concatenate([hi, zl[k], hi], axis=0))
-        y0[8 + k] = o[:by, :LANES]
-        y1[8 + k] = o[by:, LANES:]
-
-    arrive(za)
-    edge = 8 // step0
-    for c in range(edge):
-        level0_own(c)
-        level0_own(bx // step0 - edge + c)
+    i, j = grids(2 * cz, LANES)
+    pos = jnp.where(i < cz + cz // 2, i, i - 2 * cz)
+    kk = j - 2
+    top = cz + 4
+    ok = (j < top) & inside(gz * cz + kk, nz * cz)
+    k1 = pick(taps, 1, 2, pos - kk + 8, ok)
+    i, j = grids(LANES, bz)
+    fine_z = cubic(j - 2 * (i - 2), i < top)
+    put(w1h, w1l, exact(k1, fine_z))
+    ry1 = up(cy + 4, 8)
+    i, j = grids(ry1, cy + 32)
+    ok = (i < cy + 4) & inside(gy * cy + i - 2, ny * cy)
+    stack(m1, pick(taps, 1, 1, j - 16 - (i - 2) + 8, ok), 3)
+    i, j = grids(by, up(ry1, 16))
+    stack(py1, cubic(i - 2 * (j - 2), j < cy + 4), 2)
+
     arrive(z2)
     parts = []
     for e in range(fx + 5):
@@ -294,17 +300,42 @@
         pq[g] = acc
     start(yp)
 
+    start(ya[1])
     arrive(ya[0])
     start(zf[0])
-    pl.loop(edge, bx // step0 - edge, unroll=4)(level0_own)
-    arrive(ya[1])
-    start(zf[1])
-    arrive(zf[0])
-    level0_halo(0, 8)
-    level0_halo(bx - 8, 8)
-    for k in range(8):
-        level0(k)
-        level0(bx - 8 + k)
+    step0 = 4
+
+    def across(own, lo, hi):
+        rows = own.shape[0] * own.shape[1]
+        other = jnp.where(
+            mask_r, hi.reshape(rows, LANES), jnp.where(mask_l, lo.reshape(rows, LANES), 0.0)
+        )
+        v = jnp.concatenate([own.reshape(rows, LANES), other], axis=1)
+        return split(dot_right(v, (w0h, w0l)))
+
+    def level0_own(c):
+        at = pl.ds(c * step0, step0)
+        hi, lo = across(x_ref[at], l0[at], r0[at])
+        zh[at, pl.ds(0, by), :] = hi.reshape(step0, by, 2 * LANES)
+        zl[at, pl.ds(0, by), :] = lo.reshape(step0, by, 2 * LANES)
+
+    def level0_halo(x, n):
+        at = pl.ds(x, n)
+        hi, lo = across(hy[at], hl[at], hr[at])
+        zh[at, pl.ds(by, 16), :] = hi.reshape(n, 16, 2 * LANES)
+        zl[at, pl.ds(by, 16), :] = lo.reshape(n, 16, 2 * LANES)
+
+    def level0(k):
+        hi = zh[k]
+        o = mm(m0[...], jnp.concatenate([hi, zl[k], hi], axis=0))
+        y0[8 + k] = o[:by, :LANES]
+        y1[8 + k] = o[by:, LANES:]
+
+    arrive(za)
+    edge = 8 // step0
+    for c in range(edge):
+        level0_own(c)
+        level0_own(bx // step0 - edge + c)
     def spread(dim, n, ref, k0):
         out = []
         for m, d in enumerate([d for d in range(-(n - 1), n) if d]):
@@ -340,7 +371,19 @@
     xg[gx] = jnp.concatenate(own, axis=1)
     ca = spread(0, nx, lambda k: xg.at[k], 0)
     begin(ca)
+
+
+    pl.loop(edge, bx // step0 - edge, unroll=4)(level0_own)
+    arrive(ya[1])
+    start(zf[1])
+    arrive(zf[0])
+    level0_halo(0, 8)
+    level0_halo(bx - 8, 8)
+    for k in range(8):
+        level0(k)
+        level0(bx - 8 + k)
     start(xa[0])
+    start(hop1)
     arrive(zf[1])
     level0_halo(8, bx - 16)
     pl.loop(8, bx - 8, unroll=8)(level0)
@@ -351,14 +394,6 @@
         t1[p] = jnp.where(lane < cz, a, pltpu.roll(b, cz, 1))
     start(xb)
     start(xa[1])
-
-    def conv0(p):
-        acc = taps[0, 0, 0] * y0[p]
-        for t in range(1, 17):
-            acc = acc + taps[0, 0, t] * y0[p + t]
-        out_ref[p] = acc
-
-    pl.loop(8, bx - 8)(conv0)
 
     landed(ca)
     for m in range(np2 * nx):
@@ -371,21 +406,16 @@
     cb = spread(1, ny, lambda k: g2.at[gz, k], 0)
     begin(cb)
 
-    i, j = grids(2 * cz, LANES)
-    pos = jnp.where(i < cz + cz // 2, i, i - 2 * cz)
-    kk = j - 2
-    top = cz + 4
-    ok = (j < top) & inside(gz * cz + kk, nz * cz)
-    k1 = pick(taps, 1, 2, pos - kk + 8, ok)
-    i, j = grids(LANES, bz)
-    fine_z = cubic(j - 2 * (i - 2), i < top)
-    put(w1h, w1l, exact(k1, fine_z))
-    ry1 = up(cy + 4, 8)
-    i, j = grids(ry1, cy + 32)
-    ok = (i < cy + 4) & inside(gy * cy + i - 2, ny * cy)
-    stack(m1, pick(taps, 1, 1, j - 16 - (i - 2) + 8, ok), 3)
-    i, j = grids(by, up(ry1, 16))
-    stack(py1, cubic(i - 2 * (j - 2), j < cy + 4), 2)
+    def conv0(p, ts):
+        acc = None
+        for t in ts:
+            v = taps[0, 0, t] * y0[p + t]
+            acc = v if acc is None else acc + v
+        return acc
+
+    @pl.loop(8, bx - 8)
+    def _(p):
+        out_ref[p] = conv0(p, range(17))
 
     def plain(axis, level, n, pad, turned):
         i, j = grids(pad, pad)
@@ -437,6 +467,11 @@
     put(pz2, None, exact(e1_z, fine_z))
     i, j = grids(ry1, up(ty, 16))
     stack(py2, cubic((i - 2) - 2 * (j - 2), (j < ey) & (i < cy + 4) & inside(gy * cy + i - 2, ny * cy)), 2)
+    for p in range(8):
+        out_ref[p] = conv0(p, range(8 - p, 17))
+        out_ref[bx - 8 + p] = conv0(bx - 8 + p, range(16 - p))
+    arrive(hop1)
+    start(hop2)
     arrive(xb)
     n1 = half1 + 10
     to_l, to_r = there(*left).astype(F32), there(*right).astype(F32)
@@ -468,12 +503,6 @@
     landed(cb)
     cc = spread(2, nz, lambda k: g2.at[k], 0)
     begin(cc)
-    arrive(yb)
-    for q in range(0, half1 + 2, 2):
-        o = dot_left(m1, jnp.concatenate([f1[q], f1[q + 1]], axis=1), 3)
-        h1[q] = o[:, :LANES]
-        h1[q + 1] = o[:, LANES:]
-    start(zb)
     landed(cc)
     seen = lambda r: inside(gx * cx + r - 2, nx * cx).astype(F32)
     batch = max(1, min(nx * np2, 256 // n2y))
@@ -496,6 +525,12 @@
                 lane < tz, w[:ty], jnp.where(lane < 2 * tz, w[ty:2 * ty], w[2 * ty:])
             )
 
+    arrive(yb)
+    for q in range(0, half1 + 2, 2):
+        o = dot_left(m1, jnp.concatenate([f1[q], f1[q + 1]], axis=1), 3)
+        h1[q] = o[:, :LANES]
+        h1[q + 1] = o[:, LANES:]
+    start(zb)
     parts = []
     for r in range(ex):
         acc = c2[r, pl.ds(0, 1)] * y2[0]
@@ -511,13 +546,13 @@
             w = jnp.concatenate([w, jnp.zeros((fill, LANES), F32)], axis=0)
         pro.append(dot_left(py2, w, 2))
     arrive(zb)
-    near = lax.rem(lane, cz) < cz // 2
+    inner = lax.rem(lane, cz) < cz // 2
     step1 = 5 if (half1 + 2) % 5 == 0 else 1
     for c in range(0, half1 + 2, step1):
         parts = []
         for q in range(c, c + step1):
             own = h1[q]
-            other = jnp.where(near & has_r, h1r[q], jnp.where(jnp.logical_not(near) & has_l, h1l[q], 0.0))
+            other = jnp.where(inner & has_r, h1r[q], jnp.where(jnp.logical_not(inner) & has_l, h1l[q], 0.0))
             parts.append(jnp.where(lane < cz, own, pltpu.roll(other, cz, 1)))
             parts.append(jnp.where(lane < cz, pltpu.roll(own, cz, 1), other))
         v = dot_right(jnp.concatenate(parts, axis=0), (w1h, w1l))
@@ -542,10 +577,11 @@
         pr[2 * c] = o[:, :LANES]
         pr[2 * c + 1] = o[:, LANES:]
 
-    for group in xa:
+    for group in (*xa, hop2):
         arrive(group)
-    pl.loop(0, 8)(conv0)
-    pl.loop(bx - 8, bx)(conv0)
+    for p in range(8):
+        out_ref[p] = out_ref[p] + conv0(p, range(8 - p))
+        out_ref[bx - 8 + p] = out_ref[bx - 8 + p] + conv0(bx - 8 + p, range(16 - p, 17))
 
     @pl.loop(0, cx)
     def _(m):
@@ -555,7 +591,7 @@
             0.5625 * (pr[at] + pr[at + 1]) - 0.0625 * (pr[at - 1] + pr[at + 2])
         )
 
-    for group in (*ya, za, *zf, z2, yp, *xa, xb, yb, zb):
+    for group in (*ya, za, *zf, z2, yp, *xa, hop1, hop2, xb, yb, zb):
         left_over(group)
     for group in (ca, cb, cc):
         for to, _, copy, _ in group:
@@ -582,7 +618,7 @@
         pltpu.SMEM(kernel_taps.shape, F32), V(dims, F32),
         row(bx, by), row(bx, by), row(bx, 16), row(bx, 16), row(bx, 16),
         V((bx, by + 16, 2 * LANES), BF16), V((bx, by + 16, 2 * LANES), BF16),
-        row(bx + 16, by), row(bx + 16, cy),
+        row(5, by), row(bx + 16, by), row(bx + 16, cy),
         row(half1 + 2, cy), row(6, cy), row(6, cy), row(half1 + 10, cy), row(half1 + 9, cy),
         row(half1 + 2, cy + 32), row(half1 + 2, ry1), row(half1 + 2, ry1), row(half1 + 2, ry1),
         row(cx + 4, ry1), row(cx + 4, by),
@@ -603,7 +639,7 @@
         V((LANES, bz), BF16), V((ry1, 2 * up(ty, 16)), BF16),
         V((by, 2 * up(ry1, 16)), BF16),
         V((fy + 16, 2 * by), BF16), V((2 * bz, LANES), BF16),
-        dma((2,)), dma((32,)), dma((32,)), dma((3, wide)), dma((3, wide)),
+        dma((5,)), dma((40,)), dma((40,)), dma((3, wide)), dma((3, wide)),
     ]
     return pl.pallas_call(
         functools.partial(kernel, counts, dims),
@@ -614,7 +650,7 @@
         compiler_params=pltpu.CompilerParams(
             collective_id=0, has_side_effects=True, vmem_limit_bytes=105 * 2**19
         ),
-    )(kernel_taps, charges)
+    )(pltpu.with_memory_space_constraint(kernel_taps, pltpu.HBM), charges)
 
 
 def solution(mesh):

time: 33.6 us -> 27.3 us (0.81)
  Pallas kernels: 31.7 us -> 26.1 us
  local copies, waits for them, and re-layouts: 1.67 us -> 0.97 us
    pallas_call x1, Pallas kernels: 31.7 us -> 26.1 us  [per_device(): pl.pallas_call(functools.partial(kernel, counts, dims), out_shape=jax.Sha...]
    unnamed x3 -> x1, local copies, waits for them, and re-layouts: 1.67 us -> 0.97 us
where the time goes in v5:
time: 27.3 us; the launch traced here: 27 us
  Pallas kernels  26.1 us (96%)
  local copies, waits for them, and re-layouts  0.97 us (4%)
    pallas_call x1, Pallas kernels, per_device(): pl.pallas_call(functools.partial(kernel, counts, dims), out_shape=jax.Sha...  26.1 us
    unnamed x1, local copies, waits for them, and re-layouts  0.97 us

profile of v5, /device:TPU:0, one launch (start us, length us, event | category | flops | bytes accessed | tf_op | source)
XLA Modules:
  0.0 27.0 jit_solution(10606084466969086555)
XLA Ops:
  0.0 26.1 %shard_map.28 = f32[32,64,128]{2,1,0:T(8,128)S(1)} custom-call(f32[5,3,17]{2,1,0:T(4,128)} %taps_hbm.1, f32[32,64,128]{2,1,0:T(8,128)} %x_hbm.1), custom_call_target="tpu_custom_call" | custom-call | tf_op jit(solution)/shard_map/pallas_call | solution.py:644
  26.1 1.0 %copy.4 = f32[32,64,128]{2,1,0:T(8,128)} copy(f32[32,64,128]{2,1,0:T(8,128)S(1)} %shard_map.28) | data formatting | bytes 2097152

commit v6 on v5

--- a/solution.py
+++ b/solution.py
@@ -125,6 +125,8 @@
     clear(f1, (0, 1, 0), every, pl.ds(16 + cy, 16))
     clear(yu, (0, -1, 0), every)
     clear(yd, (0, 1, 0), every)
+    f1[:, pl.ds(0, 6)] = jnp.zeros((half1 + 2, 6, LANES), F32)
+    f1[:, pl.ds(cy + 26, 6)] = jnp.zeros((half1 + 2, 6, LANES), F32)
     for ref in (ua, y1):
         ref[pl.ds(0, 8)] = jnp.zeros((8,) + ref.shape[1:], F32)
         ref[pl.ds(8 + bx, 8)] = jnp.zeros((8,) + ref.shape[1:], F32)
@@ -250,8 +252,8 @@
         ]
     xb = [remote(t1.at[pl.ds(0, 6)], t1r, left), remote(t1.at[pl.ds(half1 - 4, 6)], t1l, right)]
     yb = [
-        remote(f1.at[:, pl.ds(cy, 16)], f1.at[:, pl.ds(0, 16)], ahead),
-        remote(f1.at[:, pl.ds(16, 16)], f1.at[:, pl.ds(16 + cy, 16)], behind),
+        remote(f1.at[:, pl.ds(cy + 6, 10)], f1.at[:, pl.ds(6, 10)], ahead),
+        remote(f1.at[:, pl.ds(16, 10)], f1.at[:, pl.ds(16 + cy, 10)], behind),
     ]
     zb = [remote(h1, h1l, above), remote(h1, h1r, below)]
     start(z2)
@@ -386,7 +388,7 @@
     start(hop1)
     arrive(zf[1])
     level0_halo(8, bx - 16)
-    pl.loop(8, bx - 8, unroll=8)(level0)
+    pl.loop(8, bx - 8, unroll=True)(level0)
 
     for p in range(half1 + 2):
         a = restrict_x(y1, 4 + 4 * p)
@@ -413,7 +415,7 @@
             acc = v if acc is None else acc + v
         return acc
 
-    @pl.loop(8, bx - 8)
+    @pl.loop(8, bx - 8, unroll=4)
     def _(p):
         out_ref[p] = conv0(p, range(17))
 
@@ -492,7 +494,7 @@
             sw[k - 1] = jnp.where(lane < cz, last, back)
         last = back
 
-    @pl.loop(0, half1 + 2)
+    @pl.loop(0, half1 + 2, unroll=5)
     def _(q):
         acc = taps[1, 0, 0] * e1[q]
         for t in range(1, 17):
@@ -515,7 +517,7 @@
         z2h[pl.ds(m, batch)] = hi.reshape(batch, n2y, per * LANES)
         z2l[pl.ds(m, batch)] = lo.reshape(batch, n2y, per * LANES)
 
-    @pl.loop(0, nx * np2, unroll=4)
+    @pl.loop(0, nx * np2, unroll=8)
     def _(m):
         hi = z2h[m]
         o = mm(m2[...], jnp.concatenate([hi, z2l[m], hi], axis=0))
@@ -568,7 +570,7 @@
 
     fill1 = up(ry1, 16) - ry1
 
-    @pl.loop(0, (cx + 4) // 2, unroll=5)
+    @pl.loop(0, (cx + 4) // 2, unroll=True)
     def _(c):
         v = jnp.concatenate([d1[2 * c], d1[2 * c + 1]], axis=1)
         if fill1:
@@ -577,19 +579,22 @@
         pr[2 * c] = o[:, :LANES]
         pr[2 * c + 1] = o[:, LANES:]
 
+    def finish(m):
+        at = m + 2
+        for k in range(2):
+            p = 2 * m + k
+            v = pr[at] if k == 0 else (
+                0.5625 * (pr[at] + pr[at + 1]) - 0.0625 * (pr[at - 1] + pr[at + 2])
+            )
+            if isinstance(m, int):
+                v = v + conv0(p, range(8 - p) if p < 8 else range(8 + bx - p, 17))
+            out_ref[p] = out_ref[p] + v
+
+    pl.loop(4, cx - 4, unroll=4)(finish)
     for group in (*xa, hop2):
         arrive(group)
-    for p in range(8):
-        out_ref[p] = out_ref[p] + conv0(p, range(8 - p))
-        out_ref[bx - 8 + p] = out_ref[bx - 8 + p] + conv0(bx - 8 + p, range(16 - p, 17))
-
-    @pl.loop(0, cx)
-    def _(m):
-        at = m + 2
-        out_ref[2 * m] = out_ref[2 * m] + pr[at]
-        out_ref[2 * m + 1] = out_ref[2 * m + 1] + (
-            0.5625 * (pr[at] + pr[at + 1]) - 0.0625 * (pr[at - 1] + pr[at + 2])
-        )
+    for m in (*range(4), *range(cx - 4, cx)):
+        finish(m)
 
     for group in (*ya, za, *zf, z2, yp, *xa, hop1, hop2, xb, yb, zb):
         left_over(group)

time: 27.3 us -> 26.6 us (0.974)
  Pallas kernels: 26.1 us -> 25.5 us
    pallas_call x1, Pallas kernels: 26.1 us -> 25.5 us  [per_device(): pl.pallas_call(functools.partial(kernel, counts, dims), out_shape=jax.Sha...]
where the time goes in v6:
time: 26.6 us; the launch traced here: 26.4 us
  Pallas kernels  25.5 us (96%)
  local copies, waits for them, and re-layouts  0.97 us (4%)
    pallas_call x1, Pallas kernels, per_device(): pl.pallas_call(functools.partial(kernel, counts, dims), out_shape=jax.Sha...  25.5 us
    unnamed x1, local copies, waits for them, and re-layouts  0.97 us

profile of v6, /device:TPU:0, one launch (start us, length us, event | category | flops | bytes accessed | tf_op | source)
XLA Modules:
  0.0 26.4 jit_solution(4476208443217942719)
XLA Ops:
  0.0 25.5 %shard_map.28 = f32[32,64,128]{2,1,0:T(8,128)S(1)} custom-call(f32[5,3,17]{2,1,0:T(4,128)} %taps_hbm.1, f32[32,64,128]{2,1,0:T(8,128)} %x_hbm.1), custom_call_target="tpu_custom_call" | custom-call | tf_op jit(solution)/shard_map/pallas_call | solution.py:649
  25.5 1.0 %copy.4 = f32[32,64,128]{2,1,0:T(8,128)} copy(f32[32,64,128]{2,1,0:T(8,128)S(1)} %shard_map.28) | data formatting | bytes 2097152

commit v7 on v6

--- a/solution.py
+++ b/solution.py
@@ -215,7 +215,10 @@
             remote(x_ref.at[x, pl.ds(0, 8)], hy.at[x, pl.ds(8, 8)], behind) for x in xs
         ])
         zf.append([remote(hy.at[x], hl.at[x], above) for x in xs] + [remote(hy.at[x], hr.at[x], below) for x in xs])
-    za = [remote(x_ref, l0, above), remote(x_ref, r0, below)]
+    za = [
+        [remote(x_ref.at[x], ref.at[x], d) for x in xs for ref, d in ((l0, above), (r0, below))]
+        for xs in ends
+    ]
     z2 = [remote(v2, v2l, above), remote(v2, v2r, below)]
     yp = [
         remote(pq.at[:, pl.ds(fy, 8)], yu, ahead),
@@ -258,7 +261,7 @@
     zb = [remote(h1, h1l, above), remote(h1, h1r, below)]
     start(z2)
     start(ya[0])
-    start(za)
+    start(za[0])
     loads[4].wait()
     i, j = grids(2 * bz, bz)
     pos = jnp.where(i < bz + bz // 2, i, i - 2 * bz)
@@ -302,6 +305,7 @@
         pq[g] = acc
     start(yp)
 
+    start(za[1])
     start(ya[1])
     arrive(ya[0])
     start(zf[0])
@@ -333,7 +337,7 @@
         y0[8 + k] = o[:by, :LANES]
         y1[8 + k] = o[by:, LANES:]
 
-    arrive(za)
+    arrive(za[0])
     edge = 8 // step0
     for c in range(edge):
         level0_own(c)
@@ -375,6 +379,7 @@
     begin(ca)
 
 
+    arrive(za[1])
     pl.loop(edge, bx // step0 - edge, unroll=4)(level0_own)
     arrive(ya[1])
     start(zf[1])
@@ -596,7 +601,7 @@
     for m in (*range(4), *range(cx - 4, cx)):
         finish(m)
 
-    for group in (*ya, za, *zf, z2, yp, *xa, hop1, hop2, xb, yb, zb):
+    for group in (*ya, *za, *zf, z2, yp, *xa, hop1, hop2, xb, yb, zb):
         left_over(group)
     for group in (ca, cb, cc):
         for to, _, copy, _ in group:

time: 26.6 us -> 26.6 us (level)
  no operation moved by 1% of the time
where the time goes in v7:
time: 26.6 us; the launch traced here: 26.5 us
  Pallas kernels  25.5 us (96%)
  local copies, waits for them, and re-layouts  0.97 us (4%)
    pallas_call x1, Pallas kernels, per_device(): pl.pallas_call(functools.partial(kernel, counts, dims), out_shape=jax.Sha...  25.5 us
    unnamed x1, local copies, waits for them, and re-layouts  0.97 us

profile of v7, /device:TPU:0, one launch (start us, length us, event | category | flops | bytes accessed | tf_op | source)
XLA Modules:
  0.0 26.5 jit_solution(2190759878443675754)
XLA Ops:
  0.0 25.5 %shard_map.28 = f32[32,64,128]{2,1,0:T(8,128)S(1)} custom-call(f32[5,3,17]{2,1,0:T(4,128)} %taps_hbm.1, f32[32,64,128]{2,1,0:T(8,128)} %x_hbm.1), custom_call_target="tpu_custom_call" | custom-call | tf_op jit(solution)/shard_map/pallas_call | solution.py:654
  25.5 1.0 %copy.4 = f32[32,64,128]{2,1,0:T(8,128)} copy(f32[32,64,128]{2,1,0:T(8,128)S(1)} %shard_map.28) | data formatting | bytes 2097152
